TPU v7x, 16 devices: a whole 2x2x2 slice. The times are simulated.
16 devices in a mesh: dp: 4 (over z, y), dap: 4 (over x, core).
Axes of the slice: x: 2, y: 2, z: 2, core: 2. Of those that a mesh axis runs over, the one named last changes fastest.
Arguments:
- pair_act: bfloat16 [4, 256, 256, 128], P('dp', 'dap')
- pair_mask: int32 [4, 256, 256], P('dp', 'dap')
- true_bin: int32 [4, 256, 256], P('dp', 'dap')
- msa_act: bfloat16 [4, 64, 256, 256], P('dp', None, 'dap')
- msa_true: int32 [4, 64, 256], P('dp', None, 'dap')
- bert_mask: int32 [4, 64, 256], P('dp', None, 'dap')
- w_dist: bfloat16 [128, 64], replicated
- b_dist: float32 [64], replicated
- w_msa: bfloat16 [256, 23], replicated
- b_msa: float32 [23], replicated
Outputs:
- output 1: float32 [], replicated
- output 2: bfloat16 [4, 256, 256, 128], P('dp', 'dap')
- output 3: bfloat16 [4, 64, 256, 256], P('dp', None, 'dap')
- output 4: float32 [128, 64], replicated
- output 5: float32 [64], replicated
- output 6: float32 [256, 23], replicated
- output 7: float32 [23], replicated
All inputs are finite; a program needn't handle non-finite values.
Results may differ from a plain program's by a relative error of at most 0.00736713.
Values are sent between devices in bfloat16 or wider.
A program may use at most 1 GiB of HBM per device.

v0:
```python
import jax
import jax.numpy as jnp
from jax import lax
from jax.sharding import PartitionSpec as P

LOSS_SCALE = 2.0 ** 16
DIST_WEIGHT = 0.3
value_a10 = 2.0
DIST_EPS = 1e-6
value_a7 = 1e-8


def class_terms(logits, labels):
    log_prob = jax.nn.log_softmax(logits, axis=-1)
    onehot = jax.nn.one_hot(labels, logits.shape[-1], dtype=jnp.float32)
    return -jnp.sum(log_prob * onehot, axis=-1), jnp.exp(log_prob) - onehot


def solution(mesh):
    dp_size = mesh.shape['dp']
    pair_spec = P('dp', 'dap', None, None)
    pair_int_spec = P('dp', 'dap', None)
    local_c8 = P('dp', None, 'dap', None)
    value_a12 = P('dp', None, 'dap')

    def local_step(pair_act, pair_mask, true_bin, array_b7, piece_d8, bert_mask, w_dist, b_dist, array_b5, value_a5):
        batch_total = pair_act.shape[0] * dp_size
        mask_f = pair_mask.astype(jnp.float32)
        bert_f = bert_mask.astype(jnp.float32)
        counts = lax.psum(jnp.stack([jnp.sum(mask_f, axis=(1, 2)), jnp.sum(bert_f, axis=(1, 2))]), 'dap')
        pair_den = DIST_EPS + counts[0]
        local_c7 = value_a7 + counts[1]
        pair_cols = lax.all_to_all(pair_act, 'dap', 2, 1, tiled=True)
        logits = (jnp.einsum('bijc,ck->bijk', pair_act, w_dist, preferred_element_type=jnp.float32)
                  + jnp.einsum('bjic,ck->bijk', pair_cols, w_dist, preferred_element_type=jnp.float32)
                  + b_dist)
        dist_nll, dist_diff = class_terms(logits, true_bin)
        dist_scale = LOSS_SCALE * DIST_WEIGHT / batch_total / pair_den
        grad_pair = (dist_diff * (mask_f * dist_scale[:, None, None])[..., None]).astype(jnp.bfloat16)
        array_b10 = jnp.einsum('bsrc,ck->bsrk', array_b7, array_b5, preferred_element_type=jnp.float32) + value_a5
        piece_d7, array_b8 = class_terms(array_b10, piece_d8)
        value_a9 = LOSS_SCALE * value_a10 / batch_total / local_c7
        value_a8 = (array_b8 * (bert_f * value_a9[:, None, None])[..., None]).astype(jnp.bfloat16)
        part_sums = lax.psum(jnp.stack([jnp.sum(dist_nll * mask_f, axis=(1, 2)),
                                        jnp.sum(piece_d7 * bert_f, axis=(1, 2))]), 'dap')
        protein_loss = DIST_WEIGHT * part_sums[0] / pair_den + value_a10 * part_sums[1] / local_c7
        total_loss = lax.psum(jnp.sum(protein_loss), 'dp') / batch_total
        grad_cols = lax.all_to_all(grad_pair, 'dap', 2, 1, tiled=True)
        grad_z = (jnp.einsum('bijk,ck->bijc', grad_pair, w_dist, preferred_element_type=jnp.float32)
                  + jnp.einsum('bjik,ck->bijc', grad_cols, w_dist, preferred_element_type=jnp.float32)).astype(jnp.bfloat16)
        grad_m = jnp.einsum('bsrk,ck->bsrc', value_a8, array_b5, preferred_element_type=jnp.float32).astype(jnp.bfloat16)
        weight_grads = lax.psum((
            jnp.einsum('bijc,bijk->ck', pair_act, grad_pair, preferred_element_type=jnp.float32)
            + jnp.einsum('bjic,bijk->ck', pair_cols, grad_pair, preferred_element_type=jnp.float32),
            jnp.sum(grad_pair, axis=(0, 1, 2), dtype=jnp.float32),
            jnp.einsum('bsrc,bsrk->ck', array_b7, value_a8, preferred_element_type=jnp.float32),
            jnp.sum(value_a8, axis=(0, 1, 2), dtype=jnp.float32)), ('dp', 'dap'))
        return (total_loss, grad_z, grad_m) + tuple(weight_grads)

    return jax.shard_map(local_step, mesh=mesh,
                         in_specs=(pair_spec, pair_int_spec, pair_int_spec, local_c8, value_a12, value_a12,
                                   P(), P(), P(), P()),
                         out_specs=(P(), pair_spec, local_c8, P(), P(), P(), P()),
                         check_vma=False)
```

profile of v0, /device:TPU:0, one launch (start us, length us, event | category | flops | bytes accessed | tf_op | source)
XLA Modules:
  0.0 194.8 jit_solution(9950504730099352843)
XLA Ops:
  0.6 0.0 copy-start
  0.6 7.0 %copy.21 = bf16[1,64,256,128]{3,1,0,2:T(8,128)(2,1)} copy(bf16[1,64,256,128]{3,2,1,0:T(8,128)(2,1)} %param.10) | data formatting | bytes 8388608 | tf_op args[0]
  7.7 5.0 %all-to-all-start = ((bf16[1,64,256,128]{3,1,0,2:T(8,128)(2,1)}), bf16[1,64,256,128]{3,1,0,2:T(8,128)(2,1)}, u32[]{:S(2)}, u32[]{:S(2)}) async-start(bf16[1,64,256,128]{3,1,0,2:T(8,128)(2,1)} %copy.21), calls=%async_computation | async-start | bytes 8388608 | tf_op jit(solution)/shard_map/all_to_all | solution.py:33
  12.7 0.0 copy-done
  12.7 0.0 copy-done.10
  12.7 0.0 copy-done.12
  12.7 0.0 copy-start.9
  12.7 0.0 copy-start.8
  12.8 1.8 fusion.17
  14.6 0.0 copy-done.11
  14.6 1.8 select_reduce_fusion.1
  16.3 0.0 copy-done.9
  16.4 0.6 convert_reduce_fusion.3
  17.0 0.0 copy-done.8
  17.0 5.7 %fusion.6 = f32[64,256,64]{1,2,0:T(8,128)} fusion(bf16[1,64,256,128]{3,2,1,0:T(8,128)(2,1)} %param.10, bf16[128,64]{0,1:T(8,128)(2,1)S(1)} %copy-done.8), kind=kOutput, calls=%fused_computation.8 | convolution fusion | flops 268435456 | bytes 8404992 | tf_op jit(solution)/shard_map/bijc,ck->bijk/dot_general | solution.py:34
  22.7 38.8 %all-to-all-done = bf16[1,64,256,128]{3,1,0,2:T(8,128)(2,1)} async-done(((bf16[1,64,256,128]{3,1,0,2:T(8,128)(2,1)}), bf16[1,64,256,128]{3,1,0,2:T(8,128)(2,1)}, u32[]{:S(2)}, u32[]{:S(2)}) %all-to-all-start) | async-done | bytes 4194336 | tf_op jit(solution)/shard_map/all_to_all | solution.py:33
  61.5 3.3 %copy.22 = bf16[1,64,4,64,128]{4,1,2,3,0:T(8,128)(2,1)S(1)} copy(bf16[1,64,4,64,128]{4,1,3,2,0:T(8,128)(2,1)} %bitcast.4) | data formatting | bytes 8388608 | tf_op jit(solution)/shard_map/all_to_all | solution.py:33
  64.8 0.0 copy-start.3
  64.8 0.1 copy-done.5
  65.0 0.0 copy-done.13
  65.0 1.6 fusion.55
  66.6 0.2 copy-done.3
  66.8 1.1 exponential_reduce_fusion
  67.9 1.5 select_reduce_fusion
  69.4 0.6 convert_reduce_fusion.2
  70.0 1.3 pad_maximum_fusion.1
  71.3 1.3 pad_maximum_fusion
  72.6 5.9 %all-reduce.1 = (f32[2,1]{1,0:T(2,128)S(1)}, f32[2,1]{1,0:T(2,128)S(1)}) all-reduce(f32[2,1]{1,0:T(2,128)S(1)} %pad_maximum_fusion, f32[2,1]{1,0:T(2,128)S(1)} %pad_maximum_fusion.1), channel_id=1, replica_groups=mesh['dp'=4,'dap'=4] {'dap'}, use_global_device_ids=true, to_apply=%region_8.9 | all-reduce | flops 4 | bytes 32 | tf_op jit(solution)/shard_map/psum | solution.py:44
  78.6 0.5 fusion.53
  79.8 5.2 %convert_reduce_fusion = (f32[64]{0:T(128)S(1)}, bf16[1,64,256,64]{2,3,1,0:T(8,128)(2,1)}) fusion(f32[64,256]{1,0:T(8,128)S(1)} %multiply_bitcast_fusion, s32[64,256]{1,0:T(8,128)S(1)} %bitcast.131, f32[64,256]{1,0:T(8,128)S(1)} %log.18, f32[1,64,256,64]{2,3,1,0:T(8,128)} %copy-done.1, f32[64,256]{1,0:T(8,128)S(1)} %get-tuple-element.27), kind=kLoop, calls=%fused_computation.10 | loop fusion | flops 9437120 | bytes 6553856 | tf_op jit(solution)/shard_map/reduce_sum | solution.py:55
  85.8 7.4 %copy.23 = bf16[1,64,256,64]{3,1,0,2:T(8,128)(2,1)} copy(bf16[1,64,256,64]{2,3,1,0:T(8,128)(2,1)} %get-tuple-element.20) | data formatting | bytes 4194304 | tf_op jit(solution)/shard_map/convert_element_type | solution.py:39
  93.2 5.9 %reshape.183 = bf16[4,2,131072]{2,1,0:T(2,128)(2,1)} reshape(bf16[256,1,64,64]{3,2,1,0:T(8,128)(2,1)} %bitcast.127) | data formatting | bytes 4194304
  99.1 4.5 %all-to-all-start.1 = ((bf16[4,2,131072]{2,1,0:T(2,128)(2,1)}), bf16[4,2,131072]{2,1,0:T(2,128)(2,1)}, u32[]{:S(2)}, u32[]{:S(2)}) async-start(bf16[4,2,131072]{2,1,0:T(2,128)(2,1)} %reshape.183), calls=%async_computation.1 | async-start | bytes 4194304 | tf_op jit(solution)/shard_map/all_to_all | solution.py:48
  103.6 0.4 convert_reduce_fusion.1
  104.0 0.4 fusion.41
  105.8 11.9 %psum.51 = f32[]{:T(128)} all-reduce(f32[]{:T(128)} %bitcast.18), channel_id=1, replica_groups=mesh['dp'=4,'dap'=4] {'dp'}, use_global_device_ids=true, to_apply=%region_12.13 | all-reduce | flops 1 | bytes 8 | tf_op jit(solution)/shard_map/psum | solution.py:47
  118.4 0.0 copy-start.4
  118.4 3.9 %fusion.28 = f32[64,128]{1,0:T(8,128)S(1)} fusion(bf16[256,64,128]{2,0,1:T(8,128)(2,1)} %bitcast.126, bf16[1,64,256,64]{2,3,1,0:T(8,128)(2,1)} %get-tuple-element.20), kind=kOutput, calls=%fused_computation.30 | convolution fusion | flops 268435456 | bytes 6324224 | tf_op jit(solution)/shard_map/bjic,bijk->ck/dot_general | solution.py:54
  122.3 0.7 copy-done.4
  123.1 0.9 fusion.36
  124.0 33.9 %all-reduce = (f32[128,64]{0,1:T(8,128)}, f32[64]{0:T(128)}, f32[256,23]{0,1:T(8,128)}, f32[23]{0:T(128)}) all-reduce(f32[128,64]{0,1:T(8,128)S(1)} %fusion.36, f32[64]{0:T(128)S(1)} %get-tuple-element.19, f32[256,23]{0,1:T(8,128)S(1)} %fusion.41, f32[23]{0:T(128)S(1)} %get-tuple-element.17), channel_id=1, replica_groups=mesh['dp'=4,'dap'=4] {'dp','dap'}, use_global_device_ids=true, to_apply=%region_13.14 | all-reduce | flops 14167 | bytes 113336 | tf_op jit(solution)/shard_map/psum | solution.py:52
  157.9 2.1 %convert_bitcast_fusion = bf16[1,64,64,256]{3,2,1,0:T(8,128)(2,1)} fusion(bf16[64,64,23]{1,2,0:T(8,128)(2,1)S(1)} %get-tuple-element.18, bf16[256,23]{0,1:T(8,128)(2,1)S(1)} %copy-done.10), kind=kOutput, calls=%fused_computation.24 | convolution fusion | flops 49283072 | bytes 2297344 | tf_op jit(solution)/shard_map/bsrk,ck->bsrc/dot_general | solution.py:51
  160.0 6.1 %fusion.11 = f32[64,256,128]{2,1,0:T(8,128)} fusion(bf16[1,64,256,64]{2,3,1,0:T(8,128)(2,1)} %get-tuple-element.20, bf16[128,64]{0,1:T(8,128)(2,1)S(1)} %copy-done.8), kind=kOutput, calls=%fused_computation.18 | convolution fusion | flops 268435456 | bytes 10502144 | tf_op jit(solution)/shard_map/bijk,ck->bijc/dot_general | solution.py:49
  166.1 0.0 all-to-all-done.1
  166.1 5.8 %reshape.184 = bf16[256,1,64,64]{3,2,1,0:T(8,128)(2,1)} reshape(bf16[4,2,131072]{2,1,0:T(2,128)(2,1)} %all-to-all-done.1) | data formatting | bytes 4194304
  171.9 7.5 %copy.24 = bf16[1,64,4,64,64]{1,2,4,3,0:T(4,128)(2,1)} copy(bf16[1,64,4,64,64]{4,1,3,2,0:T(8,128)(2,1)} %bitcast.128) | data formatting | bytes 4194304 | tf_op jit(solution)/shard_map/all_to_all | solution.py:48
  179.4 7.0 %reshape.177 = bf16[256,64,64]{0,2,1:T(8,128)(2,1)} reshape(bf16[1,4,64,64,64]{2,1,4,3,0:T(4,128)(2,1)} %bitcast.129) | data formatting | bytes 4194304 | tf_op jit(solution)/shard_map/reshape.28
  186.3 7.4 %fusion.2 = bf16[1,64,256,128]{3,2,1,0:T(8,128)(2,1)} fusion(f32[64,256,128]{2,1,0:T(8,128)} %fusion.11, bf16[256,64,64]{0,2,1:T(8,128)(2,1)} %reshape.177, bf16[128,64]{0,1:T(8,128)(2,1)S(1)} %copy-done.8), kind=kOutput, calls=%fused_computation.3 | convolution fusion | flops 272629760 | bytes 14696448 | tf_op jit(solution)/shard_map/bjik,ck->bijc/dot_general | solution.py:50
  (16 shorter events, 0.1 us)
Async XLA Ops:
  0.6 12.1 %copy-start = (bf16[1,64,64,256]{3,2,1,0:T(8,128)(2,1)S(1)}, bf16[1,64,64,256]{3,2,1,0:T(8,128)(2,1)}, u32[]{:S(2)}) copy-start(bf16[1,64,64,256]{3,2,1,0:T(8,128)(2,1)} %param.13) | copy-start | bytes 6291460
  7.7 5.0 %copy-start.10 = (bf16[256,23]{0,1:T(8,128)(2,1)S(1)}, bf16[256,23]{0,1:T(8,128)(2,1)}, u32[]{:S(2)}) copy-start(bf16[256,23]{0,1:T(8,128)(2,1)} %param.18) | copy-start | bytes 35332
  7.7 5.0 %copy-start.12 = (f32[23]{0:T(128)S(1)}, f32[23]{0:T(128)}, u32[]{:S(2)}) copy-start(f32[23]{0:T(128)} %param.19) | copy-start | bytes 280
  7.7 6.9 %copy-start.11 = (s32[1,64,64]{2,1,0:T(8,128)S(1)}, s32[1,64,64]{2,1,0:T(8,128)}, u32[]{:S(2)}) copy-start(s32[1,64,64]{2,1,0:T(8,128)} %param.14) | copy-start | bytes 49156
  7.7 53.8 %all-to-all-start = ((bf16[1,64,256,128]{3,1,0,2:T(8,128)(2,1)}), bf16[1,64,256,128]{3,1,0,2:T(8,128)(2,1)}, u32[]{:S(2)}, u32[]{:S(2)}) async-start(bf16[1,64,256,128]{3,1,0,2:T(8,128)(2,1)} %copy.21), calls=%async_computation | async-start | bytes 8388608 | tf_op jit(solution)/shard_map/all_to_all | solution.py:33
  12.7 3.6 %copy-start.9 = (s32[1,64,64]{2,1,0:T(8,128)S(1)}, s32[1,64,64]{2,1,0:T(8,128)}, u32[]{:S(2)}) copy-start(s32[1,64,64]{2,1,0:T(8,128)} %param.15) | copy-start | bytes 49156
  12.7 4.2 %copy-start.8 = (bf16[128,64]{0,1:T(8,128)(2,1)S(1)}, bf16[128,64]{0,1:T(8,128)(2,1)}, u32[]{:S(2)}) copy-start(bf16[128,64]{0,1:T(8,128)(2,1)} %param.16) | copy-start | bytes 49156
  61.5 3.4 %copy-start.5 = (f32[64,256,64]{1,2,0:T(8,128)S(1)}, f32[64,256,64]{1,2,0:T(8,128)}, u32[]{:S(2)}) copy-start(f32[64,256,64]{1,2,0:T(8,128)} %fusion.6) | copy-start | bytes 12582916
  61.5 3.5 %copy-start.13 = (f32[64]{0:T(128)S(1)}, f32[64]{0:T(128)}, u32[]{:S(2)}) copy-start(f32[64]{0:T(128)} %param.17) | copy-start | bytes 772
  64.8 1.9 copy-start.3
  66.8 2.6 %copy-start.1 = (f32[1,64,256,64]{2,3,1,0:T(8,128)}, f32[1,64,256,64]{2,3,1,0:T(8,128)S(1)}, u32[]{:S(2)}) copy-start(f32[1,64,256,64]{2,3,1,0:T(8,128)S(1)} %get-tuple-element.28) | copy-start | bytes 12582916
  66.8 1.1 copy-start.6
  66.8 2.6 %copy-start.7 = (s32[1,64,256]{2,1,0:T(8,128)S(1)}, s32[1,64,256]{2,1,0:T(8,128)}, u32[]{:S(2)}) copy-start(s32[1,64,256]{2,1,0:T(8,128)} %param.11) | copy-start | bytes 196612
  99.1 67.0 %all-to-all-start.1 = ((bf16[4,2,131072]{2,1,0:T(2,128)(2,1)}), bf16[4,2,131072]{2,1,0:T(2,128)(2,1)}, u32[]{:S(2)}, u32[]{:S(2)}) async-start(bf16[4,2,131072]{2,1,0:T(2,128)(2,1)} %reshape.183), calls=%async_computation.1 | async-start | bytes 4194304 | tf_op jit(solution)/shard_map/all_to_all | solution.py:48
  118.4 3.9 %copy-start.2 = (bf16[1,64,256,64]{2,3,1,0:T(8,128)(2,1)S(1)}, bf16[1,64,256,64]{2,3,1,0:T(8,128)(2,1)}, u32[]{:S(2)}) copy-start(bf16[1,64,256,64]{2,3,1,0:T(8,128)(2,1)} %get-tuple-element.20) | copy-start | bytes 6291460
  118.4 4.7 %copy-start.4 = (bf16[1,64,256,128]{3,2,1,0:T(8,128)(2,1)S(1)}, bf16[1,64,256,128]{3,2,1,0:T(8,128)(2,1)}, u32[]{:S(2)}) copy-start(bf16[1,64,256,128]{3,2,1,0:T(8,128)(2,1)} %param.10) | copy-start | bytes 12582916
where the time goes:
time: 196 us; the launch traced here: 195 us
  blocking collectives  51.8 us (26%)
  local copies, waits for them, and re-layouts  45.6 us (23%)
  waiting for transfers between devices  38.8 us (20%)
  matrix products  30 us (15%)
  other arithmetic  13.8 us (7%)
  starting transfers between devices  9.49 us (5%)
  between operations  5.42 us (3%)
    all_to_all x1, waiting for transfers between devices, local_step(): pair_cols = lax.all_to_all(pair_act, 'dap', 2, 1, tiled=True)  38.8 us
    psum x1, blocking collectives, local_step(): lax.psum((jnp.einsum('bijc,bijk->ck', pair_act, grad_pair, preferred_elem...  33.9 us
    unnamed x31, local copies, waits for them, and re-layouts  19.9 us
    psum x1, blocking collectives, local_step(): total_loss = lax.psum(jnp.sum(protein_loss), 'dp') / batch_total  11.9 us
    all_to_all x1, local copies, waits for them, and re-layouts, local_step(): grad_cols = lax.all_to_all(grad_pair, 'dap', 2, 1, tiled=True)  7.47 us
    convert_element_type x1, local copies, waits for them, and re-layouts, local_step(): (dist_diff * (mask_f * dist_scale[:, None, None])[..., None]).astype(jnp....  7.41 us
    dot_general x1, matrix products, local_step(): jnp.einsum('bjik,ck->bijc', grad_cols, w_dist, preferred_element_type=jnp...  7.35 us
    another operation x1, local copies, waits for them, and re-layouts  6.97 us
  transfers between devices with their start and end apart: 2, of which 1 were waited for; matrix products, arithmetic and copies ran while one was open for 12% of the time, Pallas kernels for 0%

commit v1 on v0

v1 whole, which is shorter than its diff:
```python
import jax
import jax.numpy as jnp
from jax import lax
from jax.experimental import pallas as pl
from jax.experimental.pallas import tpu as pltpu
from jax.sharding import PartitionSpec as P

LOSS_SCALE = 2.0 ** 16
DIST_WEIGHT = 0.3
MSA_WEIGHT = 2.0
DIST_EPS = 1e-6
MSA_EPS = 1e-8
MESH = pl.DeviceIdType.MESH
DSEM = pltpu.SemaphoreType.DMA
KEEP = True
H = 64
L = 128
N = 256
F32 = jnp.float32
BF16 = jnp.bfloat16
I32 = jnp.int32


def dot(a, b, ca, cb):
    return lax.dot_general(a, b, (((ca,), (cb,)), ((), ())), preferred_element_type=F32)


def eye(n, m):
    return lax.broadcasted_iota(I32, (n, m), 0) == lax.broadcasted_iota(I32, (n, m), 1)


def row_to_col(row, n):
    return jnp.sum(jnp.where(eye(n, row.shape[1]), row, 0.0), axis=1, keepdims=KEEP)


def col_to_row(col, m):
    return jnp.sum(jnp.where(eye(col.shape[0], m), col, 0.0), axis=0, keepdims=KEEP)


def lanes2(ref, i):
    return jnp.concatenate([ref[pl.ds(2 * i, 1), :], ref[pl.ds(2 * i + 1, 1), :]], axis=1)


def make_kernel(batch):
    def kernel(z_h, mask_h, tb_h, m_h, mt_h, bm_h, wd_h, bd_h, wm_h, bmb_h,
               loss_o, dz_o, dm_o, dwd_o, dbd_o, dwm_o, dbm_o,
               zv, mv, mask_v, tb_v, mt_v, bm_v, wd_v, bd_v, wm_v, bmb_v,
               wt2, w2, wmt, bias_c, mbias_c, lab, lts, ltr, l1n, l1f, l2n, l2f, mlab,
               cnt_s, cnt_r, rz, f0, f1, ntn, ntf, dwd_acc, dwm_acc, dbd_acc, dbm_acc, nll_acc,
               ps, pa, ph, pb, pc, pd, pf,
               lsem, cs, cr, ls, lr, zs, zr, ars, arr):
        dp = lax.axis_index("dp")
        d = lax.axis_index("dap")
        chip, core = d // 2, d % 2
        dap_peer = {1: chip * 2 + (1 - core), 2: (1 - chip) * 2 + core, 3: (1 - chip) * 2 + (1 - core)}
        pz, py = dp // 2, dp % 2
        dp_peer = {1: pz * 2 + (1 - py), 2: (1 - pz) * 2 + py, 3: (1 - pz) * 2 + (1 - py)}
        near = pl.multiple_of(chip * L, L)
        far = pl.multiple_of((1 - chip) * L, L)

        loc = []
        for n, (src, dst) in enumerate([(mask_h, mask_v), (tb_h, tb_v), (bm_h, bm_v), (mt_h, mt_v), (wd_h, wd_v),
                                        (bd_h, bd_v), (wm_h, wm_v), (bmb_h, bmb_v), (m_h, mv), (z_h, zv)]):
            c = pltpu.make_async_copy(src, dst, lsem.at[n])
            c.start()
            loc.append(c)

        bar = pltpu.get_barrier_semaphore()
        for k in (1, 2, 3):
            pl.semaphore_signal(bar, inc=1, device_id=(dp, dap_peer[k]), device_id_type=MESH)
            pl.semaphore_signal(bar, inc=1, device_id=(dp_peer[k], d), device_id_type=MESH)

        for n in range(4):
            loc[n].wait()
        maskf = mask_v[:].astype(F32)
        bertf = bm_v[:].astype(F32)
        cd = jnp.sum(jnp.sum(maskf, axis=0, keepdims=KEEP), axis=1, keepdims=KEEP)
        cm = jnp.sum(jnp.sum(bertf, axis=0, keepdims=KEEP), axis=1, keepdims=KEEP)
        cnt_s[0:8, :] = jnp.broadcast_to(cd, (8, L))
        cnt_s[8:16, :] = jnp.broadcast_to(cm, (8, L))
        labv = jnp.where(mask_v[:] > 0, tb_v[:], H)
        lab[:] = labv
        labf = labv.astype(F32)
        lts[:] = jnp.concatenate([labf, labf], axis=0).T

        pl.semaphore_wait(bar, 6)

        def rcopy(src, dst, s, r, dpi, dapi):
            return pltpu.make_async_remote_copy(src_ref=src, dst_ref=dst, send_sem=s, recv_sem=r,
                                                device_id=(dpi, dapi), device_id_type=MESH)

        sends = []
        cc, lc, zc = {}, {}, {}
        for k in (2, 3, 1):
            cc[k] = rcopy(cnt_s, cnt_r.at[k - 1], cs.at[k - 1], cr.at[k - 1], dp, dap_peer[k])
            cc[k].start()
        for k in (2, 3, 1):
            lc[k] = rcopy(lts.at[pl.ds(pl.multiple_of(H * dap_peer[k], H), H), :], ltr.at[k - 1],
                          ls.at[k - 1], lr.at[k - 1], dp, dap_peer[k])
            lc[k].start()
        for q in range(4):
            for k in (2, 3, 1):
                cols = pl.multiple_of(H * dap_peer[k] + 16 * q, 16)
                zc[k, q] = rcopy(z_h.at[:, pl.ds(cols, 16), :], rz.at[k - 1, q],
                                 zs.at[k - 1, q], zr.at[k - 1, q], dp, dap_peer[k])
                zc[k, q].start()


        for n in range(4, 8):
            loc[n].wait()
        wt = wd_v[:]
        wt2[:, 0:L] = wt
        wt2[:, L:N] = wt
        w2[0:H, :] = wt
        w2[H:L, :] = wt
        wmt[:] = jnp.zeros_like(wmt)
        wmt[0:23, :] = wm_v[:]
        bias_c[:] = jnp.broadcast_to(row_to_col(bd_v[:], H), (H, L))
        pad = lax.broadcasted_iota(I32, (32, 1), 0) >= 23
        mbias_c[:] = jnp.broadcast_to(jnp.where(pad, -1e30, row_to_col(bmb_v[:], 32)), (32, L))
        l1n[:] = lab[:, pl.ds(near, L)]
        l1f[:] = lab[:, pl.ds(far, L)]
        mlv = jnp.where(bm_v[:] > 0, mt_v[:], H)
        bm_v[:] = mlv
        mlab[:] = jnp.concatenate([bm_v[pl.ds(0, 32, stride=2), :], bm_v[pl.ds(1, 32, stride=2), :]], axis=1)
        for a in (dwd_acc, dwm_acc, dbd_acc, dbm_acc, nll_acc):
            a[:] = jnp.zeros_like(a)

        for k in (1, 2, 3):
            cc[k].wait_recv()
        tot = (cnt_s[:] + cnt_r[0]) + (cnt_r[1] + cnt_r[2])
        den_d = DIST_EPS + tot[0:1, :]
        den_m = MSA_EPS + tot[8:9, :]
        cvd = (LOSS_SCALE * DIST_WEIGHT / batch) / den_d
        cvm = (LOSS_SCALE * MSA_WEIGHT / batch) / den_m
        cd2 = jnp.concatenate([cvd, cvd], axis=1)
        cm2 = jnp.concatenate([cvm, cvm], axis=1)

        def fold(a):
            return a[:, 0:L] + a[:, L:N]


        loc[8].wait()

        def msa(i, carry):
            m = mv[pl.ds(pl.multiple_of(N * i, N), N), :]
            b = mbias_c[:]
            l = dot(wmt[:], m, 1, 1) + jnp.concatenate([b, b], axis=1)
            t = lanes2(mlab, i)
            mx = jnp.max(l, axis=0, keepdims=KEEP)
            e = jnp.exp(l - mx)
            s = jnp.sum(e, axis=0, keepdims=KEEP)
            eq = lax.broadcasted_iota(I32, (32, N), 0) == t
            mk = (t < H).astype(F32)
            c = cm2 * mk
            h = (e * (c / s) - jnp.where(eq, c, 0.0)).astype(BF16)
            lt = jnp.sum(jnp.where(eq, l, 0.0), axis=0, keepdims=KEEP)
            nll_acc[1:2, :] += fold(mk * (mx + jnp.log(s)) - lt)
            dbm_acc[:] += fold(h.astype(F32))
            dm_o[pl.ds(pl.multiple_of(N * i, N), N), :] = dot(h, wmt[:], 0, 0).astype(BF16)
            dwm_acc[:] += dot(h, m, 1, 0)
            return carry

        lax.fori_loop(0, 16, msa, 0)


        for k in (1, 2, 3):
            lc[k].wait_recv()
        sel = (lax.broadcasted_iota(I32, (H, L), 1) < H) == (core == 0)
        own_lt = lts[pl.ds(pl.multiple_of(H * d, H), H), :]
        l2n[:] = jnp.where(sel, own_lt, ltr[0]).astype(I32)
        l2f[:] = jnp.where(sel, ltr[1], ltr[2]).astype(I32)

        def swap(src, nt, q, off):
            chunk = src.astype(F32)
            f0[:] = chunk[:, 0:8, :].reshape(512, L)
            f1[:] = chunk[:, 8:16, :].reshape(512, L)
            for t in range(8):
                nt[16 * q + t, pl.ds(off, H), :] = f0[pl.ds(t, H, stride=8), :].astype(BF16)
                nt[16 * q + 8 + t, pl.ds(off, H), :] = f1[pl.ds(t, H, stride=8), :].astype(BF16)

        def tile(i, cols, nt, la, lb):
            zx = zv[pl.ds(2 * i, 2), pl.ds(cols, L), :].reshape(N, L)
            nx = nt[pl.ds(2 * i, 2), :, :].reshape(N, L)
            b = bias_c[:]
            l = dot(wt2[:], jnp.concatenate([zx, nx], axis=1), 1, 1) + jnp.concatenate([b, b], axis=1)
            t1 = lanes2(la, i)
            t2 = lanes2(lb, i)
            mx = jnp.max(l, axis=0, keepdims=KEEP)
            e = jnp.exp(l - mx)
            s = jnp.sum(e, axis=0, keepdims=KEEP)
            bins = lax.broadcasted_iota(I32, (H, N), 0)
            eq1 = bins == t1
            m1 = (t1 < H).astype(F32)
            c1 = cd2 * m1
            c2 = cd2 * (t2 < H).astype(F32)
            g1 = (e * (c1 / s) - jnp.where(eq1, c1, 0.0)).astype(BF16)
            g2 = (e * (c2 / s) - jnp.where(bins == t2, c2, 0.0)).astype(BF16)
            lt = jnp.sum(jnp.where(eq1, l, 0.0), axis=0, keepdims=KEEP)
            nll_acc[0:1, :] += fold(m1 * (mx + jnp.log(s)) - lt)
            dbd_acc[:] += fold(g1.astype(F32))
            g = jnp.concatenate([g1, g2], axis=0)
            dz_o[pl.ds(2 * i, 2), pl.ds(cols, L), :] = dot(g, w2[:], 0, 0).astype(BF16).reshape(2, L, L)
            dwd_acc[:] += dot(g, zx, 1, 0)

        own_off = pl.multiple_of(H * core, H)
        oth_off = pl.multiple_of(H * (1 - core), H)
        loc[9].wait()
        for q in range(4):
            swap(zv[:, pl.ds(pl.multiple_of(H * d + 16 * q, 16), 16), :], ntn, q, own_off)
        for q in range(4):
            zc[1, q].wait_recv()
            swap(rz[0, q], ntn, q, oth_off)

        def near_tile(i, carry):
            tile(i, near, ntn, l1n, l2n)
            return carry

        lax.fori_loop(0, 32, near_tile, 0)

        def far_tile(i, carry):
            tile(i, far, ntf, l1f, l2f)
            return carry

        for q in range(4):
            zc[2, q].wait_recv()
            swap(rz[1, q], ntf, q, own_off)
            zc[3, q].wait_recv()
            swap(rz[2, q], ntf, q, oth_off)
            lax.fori_loop(8 * q, 8 * q + 8, far_tile, 0)


        ps[0:H, :] = dwd_acc[0:H, :] + dwd_acc[H:L, :]
        ps[H:88, :] = dwm_acc[0:24, 0:L]
        ps[88:112, :] = dwm_acc[0:24, L:N]
        nd = jnp.sum(nll_acc[0:1, :], axis=1, keepdims=KEEP)
        nm = jnp.sum(nll_acc[1:2, :], axis=1, keepdims=KEEP)
        part = (DIST_WEIGHT * nd / den_d + MSA_WEIGHT * nm / den_m) / batch
        ps[112:113, :] = col_to_row(jnp.sum(dbd_acc[:], axis=1, keepdims=KEEP), L)
        ps[113:114, :] = col_to_row(jnp.sum(dbm_acc[:], axis=1, keepdims=KEEP), L)
        ps[114:115, :] = part
        ps[115:L, :] = jnp.zeros((13, L), F32)

        mine = pl.ds(pl.multiple_of(H * core, H), H)
        other = pl.ds(pl.multiple_of(H * (1 - core), H), H)
        ca = rcopy(ps.at[other, :], pa, ars.at[0], arr.at[0], dp, dap_peer[1])
        ca.start()
        ca.wait_recv()
        ph[:] = ps[mine, :] + pa[:]
        cb = {}
        for k in (3, 1, 2):
            cb[k] = rcopy(ph, pb.at[k - 1], ars.at[k], arr.at[k], dp_peer[k], d)
            cb[k].start()
        for k in (1, 2, 3):
            cb[k].wait_recv()
        pc[0] = (ph[:] + pb[0]) + (pb[1] + pb[2])
        cx = rcopy(pc.at[0], pc.at[1], ars.at[4], arr.at[4], dp, dap_peer[2])
        cx.start()
        cx.wait_recv()
        pd[:] = pc[0] + pc[1]
        ce = rcopy(pd, pf, ars.at[5], arr.at[5], dp, dap_peer[1])
        ce.start()
        ce.wait_recv()
        first = core == 0
        ra = jnp.where(first, pd[:], pf[:])
        rb = jnp.where(first, pf[:], pd[:])
        dwd_o[:] = ra
        dwm_o[:, 0:L] = rb[0:23, :]
        dwm_o[:, L:N] = rb[24:47, :]
        dbd_o[:] = rb[48:49, 0:H]
        dbm_o[:] = rb[49:50, 0:23]
        loss_o[:] = rb[50:51, 0:1]

        for k in (1, 2, 3):
            cc[k].wait_send()
            lc[k].wait_send()
            cb[k].wait_send()
            for q in range(4):
                zc[k, q].wait_send()
        ca.wait_send()
        cx.wait_send()
        ce.wait_send()

    return kernel


def flush_kernel(*refs):
    ins, outs, sem = refs[:7], refs[7:14], refs[14]
    copies = [pltpu.make_async_copy(a, b, sem.at[n]) for n, (a, b) in enumerate(zip(ins, outs))]
    for n in (1, 2, 0, 3, 4, 5, 6):
        copies[n].start()
    for c in copies:
        c.wait()


def solution(mesh):
    dp_size = mesh.shape["dp"]
    pair_spec = P("dp", "dap", None, None)
    pair_int_spec = P("dp", "dap", None)
    msa_spec = P("dp", None, "dap", None)
    msa_int_spec = P("dp", None, "dap")
    V = pltpu.VMEM

    def local_step(z, mask, tb, m, mt, bm, wd, bd, wm, bmb):
        args = (z.reshape(H, N, L), mask.reshape(H, N), tb.reshape(H, N), m.reshape(4096, N),
                mt.reshape(H, H), bm.reshape(H, H), wd.T, bd.reshape(1, H), wm.T, bmb.reshape(1, 23))
        args = tuple(pltpu.with_memory_space_constraint(a, pltpu.HBM) for a in args)
        shapes = [((1, 1), F32), ((H, N, L), BF16), ((4096, N), BF16), ((H, L), F32), ((1, H), F32),
                  ((23, N), F32), ((1, 23), F32)]
        scratch = [
            V((H, N, L), BF16), V((4096, N), BF16), V((H, N), I32), V((H, N), I32), V((H, H), I32),
            V((H, H), I32), V((H, L), BF16), V((1, H), F32), V((23, N), BF16), V((1, 23), F32),
            V((H, N), BF16), V((L, L), BF16), V((32, N), BF16), V((H, L), F32), V((32, L), F32),
            V((H, N), I32), V((N, L), F32), V((3, H, L), F32), V((H, L), I32), V((H, L), I32),
            V((H, L), I32), V((H, L), I32), V((32, L), I32),
            V((16, L), F32), V((3, 16, L), F32), V((3, 4, H, 16, L), BF16), V((512, L), F32), V((512, L), F32),
            V((H, L, L), BF16), V((H, L, L), BF16), V((L, L), F32), V((32, N), F32), V((H, L), F32),
            V((32, L), F32), V((8, L), F32),
            V((L, L), F32), V((H, L), F32), V((H, L), F32), V((3, H, L), F32), V((2, H, L), F32),
            V((H, L), F32), V((H, L), F32),
            DSEM((10,)),
            DSEM((3,)), DSEM((3,)), DSEM((3,)),
            DSEM((3,)), DSEM((3, 4)), DSEM((3, 4)),
            DSEM((6,)), DSEM((6,)),
        ]
        outs = pl.pallas_call(
            make_kernel(dp_size),
            out_shape=[pltpu.VMEM(s, t) for s, t in shapes],
            in_specs=[pl.BlockSpec(memory_space=pltpu.HBM)] * 10,
            out_specs=[pl.BlockSpec(memory_space=pltpu.VMEM)] * 7,
            scratch_shapes=scratch,
            compiler_params=pltpu.CompilerParams(collective_id=0, has_side_effects=True,
                                                 vmem_limit_bytes=44 * 1024 * 1024),
        )(*args)
        outs = pl.pallas_call(
            flush_kernel,
            out_shape=[jax.ShapeDtypeStruct(s, t) for s, t in shapes],
            in_specs=[pl.BlockSpec(memory_space=pltpu.VMEM)] * 7,
            out_specs=[pl.BlockSpec(memory_space=pl.ANY)] * 7,
            scratch_shapes=[DSEM((7,))],
            compiler_params=pltpu.CompilerParams(vmem_limit_bytes=8 * 1024 * 1024),
        )(*outs)
        loss, dz, dm, dwd, dbd, dwm, dbm = outs
        return (loss.reshape(()), dz.reshape(1, H, N, L), dm.reshape(1, H, H, N), dwd.T, dbd.reshape(H),
                dwm.T, dbm.reshape(23))

    return jax.shard_map(local_step, mesh=mesh,
                         in_specs=(pair_spec, pair_int_spec, pair_int_spec, msa_spec, msa_int_spec, msa_int_spec,
                                   P(), P(), P(), P()),
                         out_specs=(P(), pair_spec, msa_spec, P(), P(), P(), P()),
                         check_vma=False)
```

time: 196 us -> 70.1 us (0.36)
  Pallas kernels: 0 us -> 69.3 us
  blocking collectives: 51.8 us -> 0 us
  local copies, waits for them, and re-layouts: 45.6 us -> 0 us
  waiting for transfers between devices: 38.8 us -> 0 us
  matrix products: 30 us -> 0 us
  other arithmetic: 13.8 us -> 0 us
  starting transfers between devices: 9.49 us -> 0 us
  between operations: 5.42 us -> 0.64 us
    pallas_call x0 -> x2, Pallas kernels: none -> 69.3 us  [the longest x1 65.9 us: local_step(): pl.pallas_call(make_kernel(dp_size), out_shape=[pltpu.VMEM(s, t) for s, t...]
    psum x3 -> x0, blocking collectives: 51.8 us -> none  [the longest x1 33.9 us: local_step(): lax.psum((jnp.einsum('bijc,bijk->ck', pair_act, grad_pair, preferred_elem...]
    all_to_all x2 -> x0, waiting for transfers between devices: 38.8 us -> none  [the longest x1 38.8 us: local_step(): pair_cols = lax.all_to_all(pair_act, 'dap', 2, 1, tiled=True)]
    dot_general x8 -> x0, matrix products: 28.2 us -> none  [the longest x1 7.35 us: local_step(): jnp.einsum('bjik,ck->bijc', grad_cols, w_dist, preferred_element_type=jnp...]
    unnamed x31 -> x0, local copies, waits for them, and re-layouts: 19.9 us -> none
    reduce_sum x7 -> x0, other arithmetic: 11.1 us -> none  [the longest x1 5.22 us: local_step(): jnp.sum(grad_pair, axis=(0, 1, 2), dtype=jnp.float32)]
    all_to_all x2 -> x0, local copies, waits for them, and re-layouts: 10.8 us -> none  [the longest x1 7.47 us: local_step(): grad_cols = lax.all_to_all(grad_pair, 'dap', 2, 1, tiled=True)]
    all_to_all x2 -> x0, starting transfers between devices: 9.49 us -> none  [the longest x1 4.99 us: local_step(): pair_cols = lax.all_to_all(pair_act, 'dap', 2, 1, tiled=True)]
  transfers between devices with their start and end apart: 2 -> 0, of which waited for: 1 -> 0; matrix products, arithmetic and copies ran while one was open for 12% -> 0% of each run, Pallas kernels for 0% -> 0%
where the time goes in v1:
time: 70.1 us; the launch traced here: 70 us
  Pallas kernels  69.3 us (99%)
    pallas_call x1, Pallas kernels, local_step(): pl.pallas_call(make_kernel(dp_size), out_shape=[pltpu.VMEM(s, t) for s, t...  65.9 us
    pallas_call x1, Pallas kernels, local_step(): pl.pallas_call(flush_kernel, out_shape=[jax.ShapeDtypeStruct(s, t) for s,...  3.4 us

profile of v1, /device:TPU:0, one launch (start us, length us, event | category | flops | bytes accessed | tf_op | source)
XLA Modules:
  0.0 70.0 jit_solution(12489596483546512615)
XLA Ops:
  0.6 65.9 %shard_map.153 = (f32[1,1]{1,0:T(1,128)}, bf16[64,256,128]{2,1,0:T(8,128)(2,1)S(1)}, bf16[4096,256]{1,0:T(8,128)(2,1)S(1)}, f32[64,128]{1,0:T(8,128)S(1)}, f32[1...) custom-call(bf16[64,256,128]{2,1,0:T(8,128)(2,1)} %bitcast.17, s32[64,256]{1,0:T(8,128)} %bitcast.19, ...), custom_call_target="tpu_custom_call" | custom-call | tf_op jit(solution)/shard_map/pallas_call | solution.py:326
  66.6 3.4 %shard_map.154 = (f32[1,1]{1,0:T(1,128)}, bf16[64,256,128]{2,1,0:T(8,128)(2,1)}, bf16[4096,256]{1,0:T(8,128)(2,1)}, f32[64,128]{1,0:T(8,128)}, f32[1,64]{1,0:T(1...) custom-call(f32[1,1]{1,0:T(1,128)} %get-tuple-element.21.refs_0_, bf16[64,256,128]{2,1,0:T(8,128)(2,1)S(1)} %get-tuple-element.22.refs_1_, ...), custom_call_target="tpu_custom_call" | custom-call | tf_op jit(solution)/shard_map/pallas_call | solution.py:335

commit v2 on v1

--- a/solution.py
+++ b/solution.py
@@ -13,6 +13,12 @@
 MESH = pl.DeviceIdType.MESH
 DSEM = pltpu.SemaphoreType.DMA
 KEEP = True
+Q = 32
+EARLY = 2
+PEERS = (1, 2, 3)
+FAR = (2, 3)
+BOTH = (0, 1)
+QUARTERS = range(4)
 H = 64
 L = 128
 N = 256
@@ -45,10 +51,10 @@
     def kernel(z_h, mask_h, tb_h, m_h, mt_h, bm_h, wd_h, bd_h, wm_h, bmb_h,
                loss_o, dz_o, dm_o, dwd_o, dbd_o, dwm_o, dbm_o,
                zv, mv, mask_v, tb_v, mt_v, bm_v, wd_v, bd_v, wm_v, bmb_v,
-               wt2, w2, wmt, bias_c, mbias_c, lab, lts, ltr, l1n, l1f, l2n, l2f, mlab,
-               cnt_s, cnt_r, rz, f0, f1, ntn, ntf, dwd_acc, dwm_acc, dbd_acc, dbm_acc, nll_acc,
-               ps, pa, ph, pb, pc, pd, pf,
-               lsem, cs, cr, ls, lr, zs, zr, ars, arr):
+               wt2, w2, wmt, bias_c, mbias_c, lab, lts, ltp, ltr, l1n, l2n, t1o, t2o, t1r, t2r, mlab,
+               cnt_s, cnt_r, rn, rz, f0, f1, ntn, ntf, vb, vr, db, dr, dwd_acc, dwm_acc, dbd_acc, dbm_acc, nll_acc,
+               ps, pa, ph, px, pb, pc, pd, pf,
+               lsem, cs, cr, ls, lr, ns, nr, zs, zr, vs, vrs, ds, drs, ars, arr):
         dp = lax.axis_index("dp")
         d = lax.axis_index("dap")
         chip, core = d // 2, d % 2
@@ -57,6 +63,9 @@
         dp_peer = {1: pz * 2 + (1 - py), 2: (1 - pz) * 2 + py, 3: (1 - pz) * 2 + (1 - py)}
         near = pl.multiple_of(chip * L, L)
         far = pl.multiple_of((1 - chip) * L, L)
+        half = (chip, 1 - chip)
+        phalf = (1 - chip, chip)
+        base = {k: pl.multiple_of(H * dap_peer[k], H) for k in PEERS}
 
         loc = []
         for n, (src, dst) in enumerate([(mask_h, mask_v), (tb_h, tb_v), (bm_h, bm_v), (mt_h, mt_v), (wd_h, wd_v),
@@ -66,11 +75,11 @@
             loc.append(c)
 
         bar = pltpu.get_barrier_semaphore()
-        for k in (1, 2, 3):
+        for k in PEERS:
             pl.semaphore_signal(bar, inc=1, device_id=(dp, dap_peer[k]), device_id_type=MESH)
             pl.semaphore_signal(bar, inc=1, device_id=(dp_peer[k], d), device_id_type=MESH)
 
-        for n in range(4):
+        for n in QUARTERS:
             loc[n].wait()
         maskf = mask_v[:].astype(F32)
         bertf = bm_v[:].astype(F32)
@@ -82,6 +91,9 @@
         lab[:] = labv
         labf = labv.astype(F32)
         lts[:] = jnp.concatenate([labf, labf], axis=0).T
+        low = lax.broadcasted_iota(I32, (Q, L), 1) < H
+        for p in QUARTERS:
+            ltp[p] = jnp.where(low, lts[H * p:H * p + Q, :], lts[H * p + Q:H * p + H, :])
 
         pl.semaphore_wait(bar, 6)
 
@@ -95,17 +107,20 @@
             cc[k] = rcopy(cnt_s, cnt_r.at[k - 1], cs.at[k - 1], cr.at[k - 1], dp, dap_peer[k])
             cc[k].start()
         for k in (2, 3, 1):
-            lc[k] = rcopy(lts.at[pl.ds(pl.multiple_of(H * dap_peer[k], H), H), :], ltr.at[k - 1],
+            lc[k] = rcopy(ltp.at[dap_peer[k]], ltr.at[k - 1],
                           ls.at[k - 1], lr.at[k - 1], dp, dap_peer[k])
             lc[k].start()
-        for q in range(4):
-            for k in (2, 3, 1):
-                cols = pl.multiple_of(H * dap_peer[k] + 16 * q, 16)
-                zc[k, q] = rcopy(z_h.at[:, pl.ds(cols, 16), :], rz.at[k - 1, q],
-                                 zs.at[k - 1, q], zr.at[k - 1, q], dp, dap_peer[k])
-                zc[k, q].start()
-
-
+        nc = {}
+        for q in QUARTERS:
+            nc[q] = rcopy(z_h.at[:, pl.ds(pl.multiple_of(base[1] + 16 * q, 16), 16), :], rn.at[q],
+                          ns.at[q], nr.at[q], dp, dap_peer[1])
+            for k in FAR:
+                for b in BOTH:
+                    cols = pl.multiple_of(base[k] + Q * phalf[b] + 8 * q, 8)
+                    zc[k, q, b] = rcopy(z_h.at[Q * b:Q * b + Q, pl.ds(cols, 8), :], rz.at[k - 2, q, b],
+                                        zs.at[k - 2, q, b], zr.at[k - 2, q, b], dp, dap_peer[k])
+                    zc[k, q, b].start()
+            nc[q].start()
         for n in range(4, 8):
             loc[n].wait()
         wt = wd_v[:]
@@ -119,14 +134,13 @@
         pad = lax.broadcasted_iota(I32, (32, 1), 0) >= 23
         mbias_c[:] = jnp.broadcast_to(jnp.where(pad, -1e30, row_to_col(bmb_v[:], 32)), (32, L))
         l1n[:] = lab[:, pl.ds(near, L)]
-        l1f[:] = lab[:, pl.ds(far, L)]
         mlv = jnp.where(bm_v[:] > 0, mt_v[:], H)
         bm_v[:] = mlv
         mlab[:] = jnp.concatenate([bm_v[pl.ds(0, 32, stride=2), :], bm_v[pl.ds(1, 32, stride=2), :]], axis=1)
         for a in (dwd_acc, dwm_acc, dbd_acc, dbm_acc, nll_acc):
             a[:] = jnp.zeros_like(a)
 
-        for k in (1, 2, 3):
+        for k in PEERS:
             cc[k].wait_recv()
         tot = (cnt_s[:] + cnt_r[0]) + (cnt_r[1] + cnt_r[2])
         den_d = DIST_EPS + tot[0:1, :]
@@ -164,12 +178,36 @@
         lax.fori_loop(0, 16, msa, 0)
 
 
-        for k in (1, 2, 3):
+        for k in PEERS:
             lc[k].wait_recv()
-        sel = (lax.broadcasted_iota(I32, (H, L), 1) < H) == (core == 0)
+        def turn(a):
+            return pltpu.roll(a, H, 1)
+
+        def unpack(p):
+            return jnp.concatenate([jnp.where(low, p, turn(p)), jnp.where(low, turn(p), p)], axis=0)
+
+        def paired(a):
+            back = jnp.concatenate([pltpu.roll(a[8 * q:8 * q + 8, :], 4, 0) for q in QUARTERS], axis=0)
+            return jnp.where(low, a, back).astype(I32)
+
+        lane = lax.broadcasted_iota(I32, (Q, L), 1)
+        upper = (lane % H >= Q).astype(I32)
+        mine_low = upper == chip
+        peer_low = upper == 1 - chip
+        wide = lax.broadcasted_iota(I32, (H, L), 1) < H
         own_lt = lts[pl.ds(pl.multiple_of(H * d, H), H), :]
-        l2n[:] = jnp.where(sel, own_lt, ltr[0]).astype(I32)
-        l2f[:] = jnp.where(sel, ltr[1], ltr[2]).astype(I32)
+        l2n[:] = jnp.where(wide == (core == 0), own_lt, unpack(ltr[0])).astype(I32)
+        l1f = lab[:, pl.ds(far, L)].astype(F32)
+        for k in FAR:
+            a = jnp.where(wide == (dap_peer[k] % 2 == 0), l1f, turn(l1f))
+            t1o[k - 2] = paired(jnp.where(mine_low, a[0:Q, :], a[Q:H, :]))
+            got = ltr[k - 1]
+            t2o[k - 2] = paired(jnp.where(low == mine_low, got, turn(got)))
+            sent = ltp[dap_peer[k]]
+            t1r[k - 2] = paired(jnp.where(low == peer_low, sent, turn(sent)))
+            u = unpack(got)
+            u = jnp.concatenate([u, u], axis=0).T
+            t2r[k - 2] = paired(jnp.where(peer_low, u[0:Q, :], u[Q:H, :]))
 
         def swap(src, nt, q, off):
             chunk = src.astype(F32)
@@ -179,17 +217,22 @@
                 nt[16 * q + t, pl.ds(off, H), :] = f0[pl.ds(t, H, stride=8), :].astype(BF16)
                 nt[16 * q + 8 + t, pl.ds(off, H), :] = f1[pl.ds(t, H, stride=8), :].astype(BF16)
 
-        def tile(i, cols, nt, la, lb):
-            zx = zv[pl.ds(2 * i, 2), pl.ds(cols, L), :].reshape(N, L)
-            nx = nt[pl.ds(2 * i, 2), :, :].reshape(N, L)
+        bins = lax.broadcasted_iota(I32, (H, N), 0)
+
+        def softmax_terms(zx, nx):
             b = bias_c[:]
             l = dot(wt2[:], jnp.concatenate([zx, nx], axis=1), 1, 1) + jnp.concatenate([b, b], axis=1)
-            t1 = lanes2(la, i)
-            t2 = lanes2(lb, i)
             mx = jnp.max(l, axis=0, keepdims=KEEP)
             e = jnp.exp(l - mx)
             s = jnp.sum(e, axis=0, keepdims=KEEP)
-            bins = lax.broadcasted_iota(I32, (H, N), 0)
+            return l, e, s, mx + jnp.log(s)
+
+        def near_tile(i, carry):
+            zx = zv[pl.ds(2 * i, 2), pl.ds(near, L), :].reshape(N, L)
+            nx = ntn[pl.ds(2 * i, 2), :, :].reshape(N, L)
+            l, e, s, lse = softmax_terms(zx, nx)
+            t1 = lanes2(l1n, i)
+            t2 = lanes2(l2n, i)
             eq1 = bins == t1
             m1 = (t1 < H).astype(F32)
             c1 = cd2 * m1
@@ -197,38 +240,99 @@
             g1 = (e * (c1 / s) - jnp.where(eq1, c1, 0.0)).astype(BF16)
             g2 = (e * (c2 / s) - jnp.where(bins == t2, c2, 0.0)).astype(BF16)
             lt = jnp.sum(jnp.where(eq1, l, 0.0), axis=0, keepdims=KEEP)
-            nll_acc[0:1, :] += fold(m1 * (mx + jnp.log(s)) - lt)
+            nll_acc[0:1, :] += fold(m1 * lse - lt)
             dbd_acc[:] += fold(g1.astype(F32))
             g = jnp.concatenate([g1, g2], axis=0)
-            dz_o[pl.ds(2 * i, 2), pl.ds(cols, L), :] = dot(g, w2[:], 0, 0).astype(BF16).reshape(2, L, L)
+            dz_o[pl.ds(2 * i, 2), pl.ds(near, L), :] = dot(g, w2[:], 0, 0).astype(BF16).reshape(2, L, L)
             dwd_acc[:] += dot(g, zx, 1, 0)
+            return carry
+
+        def own_tiles(k, q):
+            for b in BOTH:
+                zc[k, q, b].wait_recv()
+                f0[0:N, :] = rz[k - 2, q, b].astype(F32).reshape(N, L)
+                for t in range(8):
+                    r = H * (t // 4) + Q * b
+                    ntf[k - 2, 4 * q + t % 4, r:r + Q, :] = f0[pl.ds(t, Q, stride=8), :].astype(BF16)
+
+            def body(j, carry):
+                spots = [(8 * q + 4 * u + 2 * j + tt + Q * half[b], pl.multiple_of(base[k] + Q * b, Q))
+                         for tt in BOTH for u in BOTH for b in BOTH]
+                zx = jnp.concatenate([zv[r, pl.ds(c, Q), :] for r, c in spots], axis=0)
+                nx = ntf[k - 2, pl.ds(4 * q + 2 * j, 2), :, :].reshape(N, L)
+                l, e, s, lse = softmax_terms(zx, nx)
+                t1 = lanes2(t1o.at[k - 2], 4 * q + j)
+                t2 = lanes2(t2o.at[k - 2], 4 * q + j)
+                eq1 = bins == t1
+                eq2 = bins == t2
+                m1 = (t1 < H).astype(F32)
+                m2 = (t2 < H).astype(F32)
+                v = e * (cd2 / s)
+                w = v - cd2
+                d1 = jnp.sum(jnp.where(eq1, w, 0.0), axis=0, keepdims=KEEP)
+                d2 = jnp.sum(jnp.where(eq2, w, 0.0), axis=0, keepdims=KEEP)
+                g1 = (jnp.where(eq1, w, v) * m1).astype(BF16)
+                g2 = (jnp.where(eq2, w, v) * m2).astype(BF16)
+                lt = jnp.sum(jnp.where(eq1, l, 0.0) + jnp.where(eq2, l, 0.0), axis=0, keepdims=KEEP)
+                nll_acc[0:1, :] += fold((m1 + m2) * lse - lt)
+                dbd_acc[:] += fold(g1.astype(F32) + g2.astype(F32))
+                vh = v.astype(BF16)
+                for tt in BOTH:
+                    cut = slice(L * tt, L * tt + L)
+                    vb[k - 2, q, 2 * j + tt] = vh[:, cut]
+                    db[k - 2, q, pl.ds(2 * j + tt, 1), :] = d1[:, cut]
+                    db[k - 2, q, pl.ds(4 + 2 * j + tt, 1), :] = d2[:, cut]
+                g = jnp.concatenate([g1, g2], axis=0)
+                dz = dot(g, w2[:], 0, 0).astype(BF16)
+                for n, (r, c) in enumerate(spots):
+                    dz_o[r, pl.ds(c, Q), :] = dz[Q * n:Q * n + Q, :]
+                dwd_acc[:] += dot(g, zx, 1, 0) + dot(g, nx, 1, 0)
+                return carry
+
+            lax.fori_loop(0, 2, body, 0)
+
+        vc, dc = {}, {}
+
+        def give(k, q):
+            vc[k, q] = rcopy(vb.at[k - 2, q], vr.at[k - 2, q], vs.at[k - 2, q], vrs.at[k - 2, q], dp, dap_peer[k])
+            dc[k, q] = rcopy(db.at[k - 2, q], dr.at[k - 2, q], ds.at[k - 2, q], drs.at[k - 2, q], dp, dap_peer[k])
+            vc[k, q].start()
+            dc[k, q].start()
+
+        def take(k, q):
+            vc[k, q].wait_recv()
+            dc[k, q].wait_recv()
+            for j in BOTH:
+                v = jnp.concatenate([vr[k - 2, q, 2 * j], vr[k - 2, q, 2 * j + 1]], axis=1).astype(F32)
+                gs = []
+                for table, row in ((t1r, 4 + 2 * j), (t2r, 2 * j)):
+                    t = lanes2(table.at[k - 2], 4 * q + j)
+                    on = jnp.concatenate([dr[k - 2, q, row:row + 1, :], dr[k - 2, q, row + 1:row + 2, :]], axis=1)
+                    gs.append((jnp.where(bins == t, on, v) * (t < H).astype(F32)).astype(BF16))
+                dz = dot(jnp.concatenate(gs, axis=0), w2[:], 0, 0)
+                for tt in BOTH:
+                    for u in BOTH:
+                        for f, r in ((f0, L * tt + H * u), (f1, L * tt + H * u + Q)):
+                            f[pl.ds(4 * u + 2 * j + tt, Q, stride=8), :] = dz[r:r + Q, :]
+            for b, f in ((0, f0), (1, f1)):
+                cols = pl.multiple_of(base[k] + Q * phalf[b] + 8 * q, 8)
+                dz_o[Q * b:Q * b + Q, pl.ds(cols, 8), :] = f[0:N, :].reshape(Q, 8, L).astype(BF16)
 
         own_off = pl.multiple_of(H * core, H)
         oth_off = pl.multiple_of(H * (1 - core), H)
         loc[9].wait()
-        for q in range(4):
+        for q in QUARTERS:
             swap(zv[:, pl.ds(pl.multiple_of(H * d + 16 * q, 16), 16), :], ntn, q, own_off)
-        for q in range(4):
-            zc[1, q].wait_recv()
-            swap(rz[0, q], ntn, q, oth_off)
-
-        def near_tile(i, carry):
-            tile(i, near, ntn, l1n, l2n)
-            return carry
-
+        for q in QUARTERS:
+            nc[q].wait_recv()
+            swap(rn[q], ntn, q, oth_off)
         lax.fori_loop(0, 32, near_tile, 0)
 
-        def far_tile(i, carry):
-            tile(i, far, ntf, l1f, l2f)
-            return carry
-
-        for q in range(4):
-            zc[2, q].wait_recv()
-            swap(rz[1, q], ntf, q, own_off)
-            zc[3, q].wait_recv()
-            swap(rz[2, q], ntf, q, oth_off)
-            lax.fori_loop(8 * q, 8 * q + 8, far_tile, 0)
-
+        for q in QUARTERS:
+            for k in FAR:
+                own_tiles(k, q)
+                if q < EARLY:
+                    give(k, q)
 
         ps[0:H, :] = dwd_acc[0:H, :] + dwd_acc[H:L, :]
         ps[H:88, :] = dwm_acc[0:24, 0:L]
@@ -247,19 +351,29 @@
         ca.start()
         ca.wait_recv()
         ph[:] = ps[mine, :] + pa[:]
+        cx = rcopy(ph, px, ars.at[4], arr.at[4], dp, dap_peer[2])
+        cx.start()
+        for q in range(EARLY, 4):
+            for k in FAR:
+                give(k, q)
+        for q in BOTH:
+            for k in FAR:
+                take(k, q)
+        cx.wait_recv()
+        pc[:] = ph[:] + px[:]
         cb = {}
         for k in (3, 1, 2):
-            cb[k] = rcopy(ph, pb.at[k - 1], ars.at[k], arr.at[k], dp_peer[k], d)
+            cb[k] = rcopy(pc, pb.at[k - 1], ars.at[k], arr.at[k], dp_peer[k], d)
             cb[k].start()
-        for k in (1, 2, 3):
+        for k in FAR:
+            take(k, 2)
+        for k in PEERS:
             cb[k].wait_recv()
-        pc[0] = (ph[:] + pb[0]) + (pb[1] + pb[2])
-        cx = rcopy(pc.at[0], pc.at[1], ars.at[4], arr.at[4], dp, dap_peer[2])
-        cx.start()
-        cx.wait_recv()
-        pd[:] = pc[0] + pc[1]
+        pd[:] = (pc[:] + pb[0]) + (pb[1] + pb[2])
         ce = rcopy(pd, pf, ars.at[5], arr.at[5], dp, dap_peer[1])
         ce.start()
+        for k in FAR:
+            take(k, 3)
         ce.wait_recv()
         first = core == 0
         ra = jnp.where(first, pd[:], pf[:])
@@ -271,12 +385,12 @@
         dbm_o[:] = rb[49:50, 0:23]
         loss_o[:] = rb[50:51, 0:1]
 
-        for k in (1, 2, 3):
+        for k in PEERS:
             cc[k].wait_send()
             lc[k].wait_send()
             cb[k].wait_send()
-            for q in range(4):
-                zc[k, q].wait_send()
+        for c in (*nc.values(), *zc.values(), *vc.values(), *dc.values()):
+            c.wait_send()
         ca.wait_send()
         cx.wait_send()
         ce.wait_send()
@@ -311,16 +425,16 @@
             V((H, N, L), BF16), V((4096, N), BF16), V((H, N), I32), V((H, N), I32), V((H, H), I32),
             V((H, H), I32), V((H, L), BF16), V((1, H), F32), V((23, N), BF16), V((1, 23), F32),
             V((H, N), BF16), V((L, L), BF16), V((32, N), BF16), V((H, L), F32), V((32, L), F32),
-            V((H, N), I32), V((N, L), F32), V((3, H, L), F32), V((H, L), I32), V((H, L), I32),
-            V((H, L), I32), V((H, L), I32), V((32, L), I32),
-            V((16, L), F32), V((3, 16, L), F32), V((3, 4, H, 16, L), BF16), V((512, L), F32), V((512, L), F32),
-            V((H, L, L), BF16), V((H, L, L), BF16), V((L, L), F32), V((32, N), F32), V((H, L), F32),
-            V((32, L), F32), V((8, L), F32),
-            V((L, L), F32), V((H, L), F32), V((H, L), F32), V((3, H, L), F32), V((2, H, L), F32),
+            V((H, N), I32), V((N, L), F32), V((4, Q, L), F32), V((3, Q, L), F32), V((H, L), I32), V((H, L), I32),
+            V((2, Q, L), I32), V((2, Q, L), I32), V((2, Q, L), I32), V((2, Q, L), I32), V((32, L), I32),
+            V((16, L), F32), V((3, 16, L), F32), V((4, H, 16, L), BF16), V((2, 4, 2, Q, 8, L), BF16),
+            V((512, L), F32), V((512, L), F32), V((H, L, L), BF16), V((2, 16, L, L), BF16),
+            V((2, 4, 4, H, L), BF16), V((2, 4, 4, H, L), BF16), V((2, 4, 8, L), F32), V((2, 4, 8, L), F32),
+            V((L, L), F32), V((32, N), F32), V((H, L), F32), V((32, L), F32), V((8, L), F32),
+            V((L, L), F32), V((H, L), F32), V((H, L), F32), V((H, L), F32), V((3, H, L), F32), V((H, L), F32),
             V((H, L), F32), V((H, L), F32),
-            DSEM((10,)),
-            DSEM((3,)), DSEM((3,)), DSEM((3,)),
-            DSEM((3,)), DSEM((3, 4)), DSEM((3, 4)),
+            DSEM((10,)), DSEM((3,)), DSEM((3,)), DSEM((3,)), DSEM((3,)), DSEM((4,)), DSEM((4,)),
+            DSEM((2, 4, 2)), DSEM((2, 4, 2)), DSEM((2, 4)), DSEM((2, 4)), DSEM((2, 4)), DSEM((2, 4)),
             DSEM((6,)), DSEM((6,)),
         ]
         outs = pl.pallas_call(

time: 70.1 us -> 55.8 us (0.80)
  Pallas kernels: 69.3 us -> 55.1 us
    pallas_call x1, Pallas kernels: 65.9 us -> 51.7 us  [local_step(): pl.pallas_call(make_kernel(dp_size), out_shape=[pltpu.VMEM(s, t) for s, t...]
where the time goes in v2:
time: 55.8 us; the launch traced here: 55.7 us
  Pallas kernels  55.1 us (99%)
  between operations  0.64 us (1%)
    pallas_call x1, Pallas kernels, local_step(): pl.pallas_call(make_kernel(dp_size), out_shape=[pltpu.VMEM(s, t) for s, t...  51.7 us
    pallas_call x1, Pallas kernels, local_step(): pl.pallas_call(flush_kernel, out_shape=[jax.ShapeDtypeStruct(s, t) for s,...  3.4 us

profile of v2, /device:TPU:0, one launch (start us, length us, event | category | flops | bytes accessed | tf_op | source)
XLA Modules:
  0.0 55.7 jit_solution(15467322112605089955)
XLA Ops:
  0.6 51.7 %shard_map.153 = (f32[1,1]{1,0:T(1,128)}, bf16[64,256,128]{2,1,0:T(8,128)(2,1)S(1)}, bf16[4096,256]{1,0:T(8,128)(2,1)S(1)}, f32[64,128]{1,0:T(8,128)S(1)}, f32[1...) custom-call(bf16[64,256,128]{2,1,0:T(8,128)(2,1)} %bitcast.17, s32[64,256]{1,0:T(8,128)} %bitcast.19, ...), custom_call_target="tpu_custom_call" | custom-call | tf_op jit(solution)/shard_map/pallas_call | solution.py:440
  52.3 3.4 %shard_map.154 = (f32[1,1]{1,0:T(1,128)}, bf16[64,256,128]{2,1,0:T(8,128)(2,1)}, bf16[4096,256]{1,0:T(8,128)(2,1)}, f32[64,128]{1,0:T(8,128)}, f32[1,64]{1,0:T(1...) custom-call(f32[1,1]{1,0:T(1,128)} %get-tuple-element.21.refs_0_, bf16[64,256,128]{2,1,0:T(8,128)(2,1)S(1)} %get-tuple-element.22.refs_1_, ...), custom_call_target="tpu_custom_call" | custom-call | tf_op jit(solution)/shard_map/pallas_call | solution.py:449

commit v3 on v2

--- a/solution.py
+++ b/solution.py
@@ -175,7 +175,7 @@
             dwm_acc[:] += dot(h, m, 1, 0)
             return carry
 
-        lax.fori_loop(0, 16, msa, 0)
+        lax.fori_loop(0, 16, msa, 0, unroll=4)
 
 
         for k in PEERS:
@@ -289,7 +289,7 @@
                 dwd_acc[:] += dot(g, zx, 1, 0) + dot(g, nx, 1, 0)
                 return carry
 
-            lax.fori_loop(0, 2, body, 0)
+            lax.fori_loop(0, 2, body, 0, unroll=2)
 
         vc, dc = {}, {}
 
@@ -326,7 +326,7 @@
         for q in QUARTERS:
             nc[q].wait_recv()
             swap(rn[q], ntn, q, oth_off)
-        lax.fori_loop(0, 32, near_tile, 0)
+        lax.fori_loop(0, 32, near_tile, 0, unroll=4)
 
         for q in QUARTERS:
             for k in FAR:

time: 55.8 us -> 47.9 us (0.86)
  Pallas kernels: 55.1 us -> 47.1 us
    pallas_call x1, Pallas kernels: 51.7 us -> 43.7 us  [local_step(): pl.pallas_call(make_kernel(dp_size), out_shape=[pltpu.VMEM(s, t) for s, t...]
where the time goes in v3:
time: 47.9 us; the launch traced here: 47.8 us
  Pallas kernels  47.1 us (98%)
  between operations  0.64 us (1%)
    pallas_call x1, Pallas kernels, local_step(): pl.pallas_call(make_kernel(dp_size), out_shape=[pltpu.VMEM(s, t) for s, t...  43.7 us
    pallas_call x1, Pallas kernels, local_step(): pl.pallas_call(flush_kernel, out_shape=[jax.ShapeDtypeStruct(s, t) for s,...  3.4 us

profile of v3, /device:TPU:0, one launch (start us, length us, event | category | flops | bytes accessed | tf_op | source)
XLA Modules:
  0.0 47.8 jit_solution(3160378076431236208)
XLA Ops:
  0.6 43.7 %shard_map.153 = (f32[1,1]{1,0:T(1,128)}, bf16[64,256,128]{2,1,0:T(8,128)(2,1)S(1)}, bf16[4096,256]{1,0:T(8,128)(2,1)S(1)}, f32[64,128]{1,0:T(8,128)S(1)}, f32[1...) custom-call(bf16[64,256,128]{2,1,0:T(8,128)(2,1)} %bitcast.17, s32[64,256]{1,0:T(8,128)} %bitcast.19, ...), custom_call_target="tpu_custom_call" | custom-call | tf_op jit(solution)/shard_map/pallas_call | solution.py:440
  44.4 3.4 %shard_map.154 = (f32[1,1]{1,0:T(1,128)}, bf16[64,256,128]{2,1,0:T(8,128)(2,1)}, bf16[4096,256]{1,0:T(8,128)(2,1)}, f32[64,128]{1,0:T(8,128)}, f32[1,64]{1,0:T(1...) custom-call(f32[1,1]{1,0:T(1,128)} %get-tuple-element.21.refs_0_, bf16[64,256,128]{2,1,0:T(8,128)(2,1)S(1)} %get-tuple-element.22.refs_1_, ...), custom_call_target="tpu_custom_call" | custom-call | tf_op jit(solution)/shard_map/pallas_call | solution.py:449

commit v4 on v3

--- a/solution.py
+++ b/solution.py
@@ -19,6 +19,9 @@
 FAR = (2, 3)
 BOTH = (0, 1)
 QUARTERS = range(4)
+KIB = 1024
+LAST = 3
+S = 56
 H = 64
 L = 128
 N = 256
@@ -47,12 +50,29 @@
     return jnp.concatenate([ref[pl.ds(2 * i, 1), :], ref[pl.ds(2 * i + 1, 1), :]], axis=1)
 
 
+def returned_pairs(v_ref, d_ref, mine, peers, first, w2, f0, f1):
+    bins = lax.broadcasted_iota(I32, (H, N), 0)
+    dv = d_ref[:].astype(F32)
+    for j in BOTH:
+        v = jnp.concatenate([v_ref[2 * j], v_ref[2 * j + 1]], axis=1).astype(F32)
+        gs = []
+        for table, row in ((mine, 4 + 2 * j), (peers, 2 * j)):
+            t = lanes2(table, first + j)
+            on = jnp.concatenate([dv[row:row + 1, :], dv[row + 1:row + 2, :]], axis=1)
+            gs.append((jnp.where(bins == t, on, v) * (t < H).astype(F32)).astype(BF16))
+        dz = dot(jnp.concatenate(gs, axis=0), w2[:], 0, 0)
+        for tt in BOTH:
+            for u in BOTH:
+                for f, r in ((f0, L * tt + H * u), (f1, L * tt + H * u + Q)):
+                    f[pl.ds(4 * u + 2 * j + tt, Q, stride=8), :] = dz[r:r + Q, :]
+
+
 def make_kernel(batch):
     def kernel(z_h, mask_h, tb_h, m_h, mt_h, bm_h, wd_h, bd_h, wm_h, bmb_h,
-               loss_o, dz_o, dm_o, dwd_o, dbd_o, dwm_o, dbm_o,
+               loss_o, dz_o, dm_o, dwd_o, dbd_o, dwm_o, dbm_o, vl_o, dl_o, tl_o, w2,
                zv, mv, mask_v, tb_v, mt_v, bm_v, wd_v, bd_v, wm_v, bmb_v,
-               wt2, w2, wmt, bias_c, mbias_c, lab, lts, ltp, ltr, l1n, l2n, t1o, t2o, t1r, t2r, mlab,
-               cnt_s, cnt_r, rn, rz, f0, f1, ntn, ntf, vb, vr, db, dr, dwd_acc, dwm_acc, dbd_acc, dbm_acc, nll_acc,
+               wt2, wmt, wmn, bias_c, mbias_c, lab, lts, ltp, ltr, l1n, l2n, t1o, t2o, t1r, t2r, mlab,
+               cnt_s, cnt_r, rn, rz, f0, f1, ntn, ntf, vb, vr, db, dbh, dr, dwd_acc, dwm_acc, dbd_acc, dbm_acc, nll_acc,
                ps, pa, ph, px, pb, pc, pd, pf,
                lsem, cs, cr, ls, lr, ns, nr, zs, zr, vs, vrs, ds, drs, ars, arr):
         dp = lax.axis_index("dp")
@@ -124,12 +144,14 @@
         for n in range(4, 8):
             loc[n].wait()
         wt = wd_v[:]
-        wt2[:, 0:L] = wt
-        wt2[:, L:N] = wt
+        nat = wt.astype(F32).T.astype(BF16)
+        wt2[0:L, :] = nat
+        wt2[L:N, :] = nat
         w2[0:H, :] = wt
         w2[H:L, :] = wt
         wmt[:] = jnp.zeros_like(wmt)
         wmt[0:23, :] = wm_v[:]
+        wmn[:] = wmt[:].astype(F32).T.astype(BF16)
         bias_c[:] = jnp.broadcast_to(row_to_col(bd_v[:], H), (H, L))
         pad = lax.broadcasted_iota(I32, (32, 1), 0) >= 23
         mbias_c[:] = jnp.broadcast_to(jnp.where(pad, -1e30, row_to_col(bmb_v[:], 32)), (32, L))
@@ -159,7 +181,7 @@
         def msa(i, carry):
             m = mv[pl.ds(pl.multiple_of(N * i, N), N), :]
             b = mbias_c[:]
-            l = dot(wmt[:], m, 1, 1) + jnp.concatenate([b, b], axis=1)
+            l = dot(m, wmn[:], 1, 0).T + jnp.concatenate([b, b], axis=1)
             t = lanes2(mlab, i)
             mx = jnp.max(l, axis=0, keepdims=KEEP)
             e = jnp.exp(l - mx)
@@ -208,6 +230,8 @@
             u = unpack(got)
             u = jnp.concatenate([u, u], axis=0).T
             t2r[k - 2] = paired(jnp.where(peer_low, u[0:Q, :], u[Q:H, :]))
+            tl_o[0, k - 2] = t1r[k - 2, 8 * LAST:Q, :]
+            tl_o[1, k - 2] = t2r[k - 2, 8 * LAST:Q, :]
 
         def swap(src, nt, q, off):
             chunk = src.astype(F32)
@@ -221,7 +245,7 @@
 
         def softmax_terms(zx, nx):
             b = bias_c[:]
-            l = dot(wt2[:], jnp.concatenate([zx, nx], axis=1), 1, 1) + jnp.concatenate([b, b], axis=1)
+            l = dot(jnp.concatenate([zx, nx], axis=1), wt2[:], 1, 0).T + jnp.concatenate([b, b], axis=1)
             mx = jnp.max(l, axis=0, keepdims=KEEP)
             e = jnp.exp(l - mx)
             s = jnp.sum(e, axis=0, keepdims=KEEP)
@@ -290,30 +314,21 @@
                 return carry
 
             lax.fori_loop(0, 2, body, 0, unroll=2)
+            dbh[k - 2, q] = db[k - 2, q].astype(BF16)
 
         vc, dc = {}, {}
 
         def give(k, q):
-            vc[k, q] = rcopy(vb.at[k - 2, q], vr.at[k - 2, q], vs.at[k - 2, q], vrs.at[k - 2, q], dp, dap_peer[k])
-            dc[k, q] = rcopy(db.at[k - 2, q], dr.at[k - 2, q], ds.at[k - 2, q], drs.at[k - 2, q], dp, dap_peer[k])
+            v_to, d_to = (vr.at[k - 2, q], dr.at[k - 2, q]) if q < LAST else (vl_o.at[k - 2], dl_o.at[k - 2])
+            vc[k, q] = rcopy(vb.at[k - 2, q], v_to, vs.at[k - 2, q], vrs.at[k - 2, q], dp, dap_peer[k])
+            dc[k, q] = rcopy(dbh.at[k - 2, q], d_to, ds.at[k - 2, q], drs.at[k - 2, q], dp, dap_peer[k])
             vc[k, q].start()
             dc[k, q].start()
 
         def take(k, q):
             vc[k, q].wait_recv()
             dc[k, q].wait_recv()
-            for j in BOTH:
-                v = jnp.concatenate([vr[k - 2, q, 2 * j], vr[k - 2, q, 2 * j + 1]], axis=1).astype(F32)
-                gs = []
-                for table, row in ((t1r, 4 + 2 * j), (t2r, 2 * j)):
-                    t = lanes2(table.at[k - 2], 4 * q + j)
-                    on = jnp.concatenate([dr[k - 2, q, row:row + 1, :], dr[k - 2, q, row + 1:row + 2, :]], axis=1)
-                    gs.append((jnp.where(bins == t, on, v) * (t < H).astype(F32)).astype(BF16))
-                dz = dot(jnp.concatenate(gs, axis=0), w2[:], 0, 0)
-                for tt in BOTH:
-                    for u in BOTH:
-                        for f, r in ((f0, L * tt + H * u), (f1, L * tt + H * u + Q)):
-                            f[pl.ds(4 * u + 2 * j + tt, Q, stride=8), :] = dz[r:r + Q, :]
+            returned_pairs(vr.at[k - 2, q], dr.at[k - 2, q], t1r.at[k - 2], t2r.at[k - 2], 4 * q, w2, f0, f1)
             for b, f in ((0, f0), (1, f1)):
                 cols = pl.multiple_of(base[k] + Q * phalf[b] + 8 * q, 8)
                 dz_o[Q * b:Q * b + Q, pl.ds(cols, 8), :] = f[0:N, :].reshape(Q, 8, L).astype(BF16)
@@ -335,18 +350,19 @@
                     give(k, q)
 
         ps[0:H, :] = dwd_acc[0:H, :] + dwd_acc[H:L, :]
-        ps[H:88, :] = dwm_acc[0:24, 0:L]
-        ps[88:112, :] = dwm_acc[0:24, L:N]
+        ps[H:87, :] = dwm_acc[0:23, 0:L]
+        ps[87:110, :] = dwm_acc[0:23, L:N]
         nd = jnp.sum(nll_acc[0:1, :], axis=1, keepdims=KEEP)
         nm = jnp.sum(nll_acc[1:2, :], axis=1, keepdims=KEEP)
         part = (DIST_WEIGHT * nd / den_d + MSA_WEIGHT * nm / den_m) / batch
-        ps[112:113, :] = col_to_row(jnp.sum(dbd_acc[:], axis=1, keepdims=KEEP), L)
-        ps[113:114, :] = col_to_row(jnp.sum(dbm_acc[:], axis=1, keepdims=KEEP), L)
-        ps[114:115, :] = part
-        ps[115:L, :] = jnp.zeros((13, L), F32)
-
-        mine = pl.ds(pl.multiple_of(H * core, H), H)
-        other = pl.ds(pl.multiple_of(H * (1 - core), H), H)
+        dbd = col_to_row(jnp.sum(dbd_acc[:], axis=1, keepdims=KEEP), L)
+        dbm = col_to_row(jnp.sum(dbm_acc[:], axis=1, keepdims=KEEP), L)
+        end = lax.broadcasted_iota(I32, (1, L), 1) == L - 1
+        ps[110:111, :] = dbd + turn(dbm) + jnp.where(end, part, 0.0)
+        ps[111:112, :] = jnp.zeros((1, L), F32)
+
+        mine = pl.ds(pl.multiple_of(S * core, S), S)
+        other = pl.ds(pl.multiple_of(S * (1 - core), S), S)
         ca = rcopy(ps.at[other, :], pa, ars.at[0], arr.at[0], dp, dap_peer[1])
         ca.start()
         ca.wait_recv()
@@ -369,21 +385,22 @@
             take(k, 2)
         for k in PEERS:
             cb[k].wait_recv()
-        pd[:] = (pc[:] + pb[0]) + (pb[1] + pb[2])
-        ce = rcopy(pd, pf, ars.at[5], arr.at[5], dp, dap_peer[1])
+        total = (pc[:] + pb[0]) + (pb[1] + pb[2])
+        pd[:] = total
+        pf[mine, :] = total
+        ce = rcopy(pd, pf.at[mine, :], ars.at[5], arr.at[5], dp, dap_peer[1])
         ce.start()
         for k in FAR:
-            take(k, 3)
+            vc[k, LAST].wait_recv()
+            dc[k, LAST].wait_recv()
         ce.wait_recv()
-        first = core == 0
-        ra = jnp.where(first, pd[:], pf[:])
-        rb = jnp.where(first, pf[:], pd[:])
-        dwd_o[:] = ra
-        dwm_o[:, 0:L] = rb[0:23, :]
-        dwm_o[:, L:N] = rb[24:47, :]
-        dbd_o[:] = rb[48:49, 0:H]
-        dbm_o[:] = rb[49:50, 0:23]
-        loss_o[:] = rb[50:51, 0:1]
+        dwd_o[:] = pf[0:H, :]
+        dwm_o[:, 0:L] = pf[H:87, :]
+        dwm_o[:, L:N] = pf[87:110, :]
+        row = pf[110:111, :]
+        dbd_o[:] = row[:, 0:H]
+        dbm_o[:] = turn(row)[:, 0:23]
+        loss_o[:] = pltpu.roll(row, 1, 1)[:, 0:1]
 
         for k in PEERS:
             cc[k].wait_send()
@@ -398,11 +415,40 @@
     return kernel
 
 
-def flush_kernel(*refs):
-    ins, outs, sem = refs[:7], refs[7:14], refs[14]
-    copies = [pltpu.make_async_copy(a, b, sem.at[n]) for n, (a, b) in enumerate(zip(ins, outs))]
-    for n in (1, 2, 0, 3, 4, 5, 6):
-        copies[n].start()
+def flush_kernel(loss_i, dz_i, dm_i, dwd_i, dbd_i, dwm_i, dbm_i, vl, dl, tl, w2,
+                 loss_o, dz_o, dm_o, dwd_o, dbd_o, dwm_o, dbm_o, f0, f1, late, sem):
+    d = lax.axis_index("dap")
+    chip, core = d // 2, d % 2
+    phalf = (1 - chip, chip)
+    copies = []
+
+    def put(src, dst):
+        c = pltpu.make_async_copy(src, dst, sem.at[len(copies)])
+        c.start()
+        copies.append(c)
+
+    def put_dz(r, rows, c, cols):
+        put(dz_i.at[pl.ds(r, rows), pl.ds(c, cols), :], dz_o.at[pl.ds(r, rows), pl.ds(c, cols), :])
+
+    for n in QUARTERS:
+        put_dz(16 * n, 16, pl.multiple_of(L * chip, L), L)
+    spots = {}
+    for k, there in ((0, core), (1, 1 - core)):
+        start = pl.multiple_of((1 - chip) * L + H * there, H)
+        for b in BOTH:
+            mid = pl.multiple_of(start + Q * phalf[b], Q)
+            put_dz(Q * b, Q, mid, 24)
+            put_dz(Q * b, Q, pl.multiple_of(start + Q * phalf[1 - b], Q), Q)
+            spots[k, b] = pl.multiple_of(mid + 24, 8)
+    for n in QUARTERS:
+        put(dm_i.at[pl.ds(KIB * n, KIB), :], dm_o.at[pl.ds(KIB * n, KIB), :])
+    for src, dst in ((loss_i, loss_o), (dwd_i, dwd_o), (dbd_i, dbd_o), (dwm_i, dwm_o), (dbm_i, dbm_o)):
+        put(src, dst)
+    for k in BOTH:
+        returned_pairs(vl.at[k], dl.at[k], tl.at[0, k], tl.at[1, k], 0, w2, f0, f1)
+        for b, f in ((0, f0), (1, f1)):
+            late[k, b] = f[:].reshape(Q, 8, L).astype(BF16)
+            put(late.at[k, b], dz_o.at[pl.ds(Q * b, Q), pl.ds(spots[k, b], 8), :])
     for c in copies:
         c.wait()
 
@@ -422,37 +468,40 @@
         shapes = [((1, 1), F32), ((H, N, L), BF16), ((4096, N), BF16), ((H, L), F32), ((1, H), F32),
                   ((23, N), F32), ((1, 23), F32)]
         scratch = [
-            V((H, N, L), BF16), V((4096, N), BF16), V((H, N), I32), V((H, N), I32), V((H, H), I32),
+            V((H, N, L), BF16), V((4096, N), BF16), *[V((H, N), I32)] * 2, V((H, H), I32),
             V((H, H), I32), V((H, L), BF16), V((1, H), F32), V((23, N), BF16), V((1, 23), F32),
-            V((H, N), BF16), V((L, L), BF16), V((32, N), BF16), V((H, L), F32), V((32, L), F32),
+            V((N, H), BF16), V((32, N), BF16), V((N, 32), BF16), V((H, L), F32), V((32, L), F32),
             V((H, N), I32), V((N, L), F32), V((4, Q, L), F32), V((3, Q, L), F32), V((H, L), I32), V((H, L), I32),
-            V((2, Q, L), I32), V((2, Q, L), I32), V((2, Q, L), I32), V((2, Q, L), I32), V((32, L), I32),
+            *[V((2, Q, L), I32)] * 4, V((32, L), I32),
             V((16, L), F32), V((3, 16, L), F32), V((4, H, 16, L), BF16), V((2, 4, 2, Q, 8, L), BF16),
             V((512, L), F32), V((512, L), F32), V((H, L, L), BF16), V((2, 16, L, L), BF16),
-            V((2, 4, 4, H, L), BF16), V((2, 4, 4, H, L), BF16), V((2, 4, 8, L), F32), V((2, 4, 8, L), F32),
+            V((2, 4, 4, H, L), BF16), V((2, 3, 4, H, L), BF16), V((2, 4, 8, L), F32), V((2, 4, 8, L), BF16), V((2, 3, 8, L), BF16),
             V((L, L), F32), V((32, N), F32), V((H, L), F32), V((32, L), F32), V((8, L), F32),
-            V((L, L), F32), V((H, L), F32), V((H, L), F32), V((H, L), F32), V((3, H, L), F32), V((H, L), F32),
-            V((H, L), F32), V((H, L), F32),
-            DSEM((10,)), DSEM((3,)), DSEM((3,)), DSEM((3,)), DSEM((3,)), DSEM((4,)), DSEM((4,)),
-            DSEM((2, 4, 2)), DSEM((2, 4, 2)), DSEM((2, 4)), DSEM((2, 4)), DSEM((2, 4)), DSEM((2, 4)),
+            V((2 * S, L), F32), V((S, L), F32), V((S, L), F32), V((S, L), F32), V((3, S, L), F32), V((S, L), F32),
+            V((S, L), F32), V((2 * S, L), F32),
+            DSEM((10,)), *[DSEM((3,))] * 4, DSEM((4,)), DSEM((4,)),
+            *[DSEM((2, 4, 2))] * 2, *[DSEM((2, 4))] * 4,
             DSEM((6,)), DSEM((6,)),
         ]
+        extra = [((2, 4, H, L), BF16), ((2, 8, L), BF16), ((2, 2, 8, L), I32), ((L, L), BF16)]
+        vmem = [pl.BlockSpec(memory_space=pltpu.VMEM)]
+        hbm = [pl.BlockSpec(memory_space=pltpu.HBM)]
         outs = pl.pallas_call(
             make_kernel(dp_size),
-            out_shape=[pltpu.VMEM(s, t) for s, t in shapes],
-            in_specs=[pl.BlockSpec(memory_space=pltpu.HBM)] * 10,
-            out_specs=[pl.BlockSpec(memory_space=pltpu.VMEM)] * 7,
+            out_shape=[pltpu.VMEM(s, t) for s, t in shapes + extra],
+            in_specs=hbm * 10,
+            out_specs=vmem * 11,
             scratch_shapes=scratch,
             compiler_params=pltpu.CompilerParams(collective_id=0, has_side_effects=True,
-                                                 vmem_limit_bytes=44 * 1024 * 1024),
+                                                 vmem_limit_bytes=44 * KIB * KIB),
         )(*args)
         outs = pl.pallas_call(
             flush_kernel,
             out_shape=[jax.ShapeDtypeStruct(s, t) for s, t in shapes],
-            in_specs=[pl.BlockSpec(memory_space=pltpu.VMEM)] * 7,
-            out_specs=[pl.BlockSpec(memory_space=pl.ANY)] * 7,
-            scratch_shapes=[DSEM((7,))],
-            compiler_params=pltpu.CompilerParams(vmem_limit_bytes=8 * 1024 * 1024),
+            in_specs=vmem * 11,
+            out_specs=hbm * 7,
+            scratch_shapes=[V((N, L), F32), V((N, L), F32), V((2, 2, Q, 8, L), BF16), DSEM((25,))],
+            compiler_params=pltpu.CompilerParams(vmem_limit_bytes=8 * KIB * KIB),
         )(*outs)
         loss, dz, dm, dwd, dbd, dwm, dbm = outs
         return (loss.reshape(()), dz.reshape(1, H, N, L), dm.reshape(1, H, H, N), dwd.T, dbd.reshape(H),

time: 47.9 us -> 47.3 us (0.987)
  Pallas kernels: 47.1 us -> 46.5 us
    pallas_call x1, Pallas kernels: 43.7 us -> 42.9 us  [local_step(): pl.pallas_call(make_kernel(dp_size), out_shape=[pltpu.VMEM(s, t) for s, t...]
where the time goes in v4:
time: 47.3 us; the launch traced here: 47.2 us
  Pallas kernels  46.5 us (98%)
  between operations  0.64 us (1%)
    pallas_call x1, Pallas kernels, local_step(): pl.pallas_call(make_kernel(dp_size), out_shape=[pltpu.VMEM(s, t) for s, t...  42.9 us
    pallas_call x1, Pallas kernels, local_step(): pl.pallas_call(flush_kernel, out_shape=[jax.ShapeDtypeStruct(s, t) for s,...  3.61 us

profile of v4, /device:TPU:0, one launch (start us, length us, event | category | flops | bytes accessed | tf_op | source)
XLA Modules:
  0.0 47.2 jit_solution(7349540932501284712)
XLA Ops:
  0.6 42.9 %shard_map.153 = (f32[1,1]{1,0:T(1,128)}, bf16[64,256,128]{2,1,0:T(8,128)(2,1)S(1)}, bf16[4096,256]{1,0:T(8,128)(2,1)S(1)}, f32[64,128]{1,0:T(8,128)S(1)}, f32[1...) custom-call(bf16[64,256,128]{2,1,0:T(8,128)(2,1)} %bitcast.17, ...), custom_call_target="tpu_custom_call" | custom-call | tf_op jit(solution)/shard_map/pallas_call | solution.py:489
  43.5 3.6 %shard_map.154 = (f32[1,1]{1,0:T(1,128)}, bf16[64,256,128]{2,1,0:T(8,128)(2,1)}, bf16[4096,256]{1,0:T(8,128)(2,1)}, f32[64,128]{1,0:T(8,128)}, f32[1,64]{1,0:T(1...) custom-call(f32[1,1]{1,0:T(1,128)} %get-tuple-element.25.loss_i, bf16[64,256,128]{2,1,0:T(8,128)(2,1)S(1)} %get-tuple-element.26.dz_i, ...), custom_call_target="tpu_custom_call" | custom-call | tf_op jit(solution)/shard_map/pallas_call | solution.py:498

commit v5 on v4

--- a/solution.py
+++ b/solution.py
@@ -14,7 +14,7 @@
 DSEM = pltpu.SemaphoreType.DMA
 KEEP = True
 Q = 32
-EARLY = 2
+EARLY = 4
 PEERS = (1, 2, 3)
 FAR = (2, 3)
 BOTH = (0, 1)
@@ -73,7 +73,7 @@
                zv, mv, mask_v, tb_v, mt_v, bm_v, wd_v, bd_v, wm_v, bmb_v,
                wt2, wmt, wmn, bias_c, mbias_c, lab, lts, ltp, ltr, l1n, l2n, t1o, t2o, t1r, t2r, mlab,
                cnt_s, cnt_r, rn, rz, f0, f1, ntn, ntf, vb, vr, db, dbh, dr, dwd_acc, dwm_acc, dbd_acc, dbm_acc, nll_acc,
-               ps, pa, ph, px, pb, pc, pd, pf,
+               ps, pa, ph, px, pb, pc, pf,
                lsem, cs, cr, ls, lr, ns, nr, zs, zr, vs, vrs, ds, drs, ars, arr):
         dp = lax.axis_index("dp")
         d = lax.axis_index("dap")
@@ -97,7 +97,9 @@
         bar = pltpu.get_barrier_semaphore()
         for k in PEERS:
             pl.semaphore_signal(bar, inc=1, device_id=(dp, dap_peer[k]), device_id_type=MESH)
-            pl.semaphore_signal(bar, inc=1, device_id=(dp_peer[k], d), device_id_type=MESH)
+        for k in (1, 2):
+            for there in (d, dap_peer[1]):
+                pl.semaphore_signal(bar, inc=1, device_id=(dp_peer[k], there), device_id_type=MESH)
 
         for n in QUARTERS:
             loc[n].wait()
@@ -115,7 +117,7 @@
         for p in QUARTERS:
             ltp[p] = jnp.where(low, lts[H * p:H * p + Q, :], lts[H * p + Q:H * p + H, :])
 
-        pl.semaphore_wait(bar, 6)
+        pl.semaphore_wait(bar, 7)
 
         def rcopy(src, dst, s, r, dpi, dapi):
             return pltpu.make_async_remote_copy(src_ref=src, dst_ref=dst, send_sem=s, recv_sem=r,
@@ -346,7 +348,7 @@
         for q in QUARTERS:
             for k in FAR:
                 own_tiles(k, q)
-                if q < EARLY:
+                if 2 * q + k - 2 < EARLY:
                     give(k, q)
 
         ps[0:H, :] = dwd_acc[0:H, :] + dwd_acc[H:L, :]
@@ -363,37 +365,41 @@
 
         mine = pl.ds(pl.multiple_of(S * core, S), S)
         other = pl.ds(pl.multiple_of(S * (1 - core), S), S)
-        ca = rcopy(ps.at[other, :], pa, ars.at[0], arr.at[0], dp, dap_peer[1])
-        ca.start()
-        ca.wait_recv()
-        ph[:] = ps[mine, :] + pa[:]
-        cx = rcopy(ph, px, ars.at[4], arr.at[4], dp, dap_peer[2])
+        def trio(halves, src, dst, first, k):
+            there = ((dp, dap_peer[1]), (dp_peer[k], d), (dp_peer[k], dap_peer[1]))
+            group = [rcopy(src.at[rows, :], dst.at[n], ars.at[first + n], arr.at[first + n], *to)
+                     for n, (rows, to) in enumerate(zip(halves, there))]
+            for c in group:
+                c.start()
+            return group
+
+        sums = trio((other, mine, other), ps, pa, 0, 1)
+        for c in sums:
+            c.wait_recv()
+        ph[:] = (ps[mine, :] + pa[0]) + (pa[1] + pa[2])
+        cx = rcopy(ph, px, ars.at[6], arr.at[6], dp, dap_peer[2])
         cx.start()
-        for q in range(EARLY, 4):
+        for q in QUARTERS:
             for k in FAR:
-                give(k, q)
-        for q in BOTH:
-            for k in FAR:
-                take(k, q)
+                if 2 * q + k - 2 >= EARLY:
+                    give(k, q)
+        for k in FAR:
+            take(k, 0)
         cx.wait_recv()
         pc[:] = ph[:] + px[:]
-        cb = {}
-        for k in (3, 1, 2):
-            cb[k] = rcopy(pc, pb.at[k - 1], ars.at[k], arr.at[k], dp_peer[k], d)
-            cb[k].start()
+        everything = pl.ds(0, S)
+        last_sums = trio((everything,) * 3, pc, pb, 3, 2)
+        for k in FAR:
+            take(k, 1)
+        for c in last_sums:
+            c.wait_recv()
+        pf[mine, :] = pc[:] + pb[1]
+        pf[other, :] = pb[0] + pb[2]
         for k in FAR:
             take(k, 2)
-        for k in PEERS:
-            cb[k].wait_recv()
-        total = (pc[:] + pb[0]) + (pb[1] + pb[2])
-        pd[:] = total
-        pf[mine, :] = total
-        ce = rcopy(pd, pf.at[mine, :], ars.at[5], arr.at[5], dp, dap_peer[1])
-        ce.start()
         for k in FAR:
             vc[k, LAST].wait_recv()
             dc[k, LAST].wait_recv()
-        ce.wait_recv()
         dwd_o[:] = pf[0:H, :]
         dwm_o[:, 0:L] = pf[H:87, :]
         dwm_o[:, L:N] = pf[87:110, :]
@@ -405,12 +411,9 @@
         for k in PEERS:
             cc[k].wait_send()
             lc[k].wait_send()
-            cb[k].wait_send()
-        for c in (*nc.values(), *zc.values(), *vc.values(), *dc.values()):
+        for c in (*nc.values(), *zc.values(), *vc.values(), *dc.values(), *sums, *last_sums):
             c.wait_send()
-        ca.wait_send()
         cx.wait_send()
-        ce.wait_send()
 
     return kernel
 
@@ -477,11 +480,11 @@
             V((512, L), F32), V((512, L), F32), V((H, L, L), BF16), V((2, 16, L, L), BF16),
             V((2, 4, 4, H, L), BF16), V((2, 3, 4, H, L), BF16), V((2, 4, 8, L), F32), V((2, 4, 8, L), BF16), V((2, 3, 8, L), BF16),
             V((L, L), F32), V((32, N), F32), V((H, L), F32), V((32, L), F32), V((8, L), F32),
-            V((2 * S, L), F32), V((S, L), F32), V((S, L), F32), V((S, L), F32), V((3, S, L), F32), V((S, L), F32),
-            V((S, L), F32), V((2 * S, L), F32),
+            V((2 * S, L), F32), V((3, S, L), F32), V((S, L), F32), V((S, L), F32), V((3, S, L), F32), V((S, L), F32),
+            V((2 * S, L), F32),
             DSEM((10,)), *[DSEM((3,))] * 4, DSEM((4,)), DSEM((4,)),
             *[DSEM((2, 4, 2))] * 2, *[DSEM((2, 4))] * 4,
-            DSEM((6,)), DSEM((6,)),
+            DSEM((7,)), DSEM((7,)),
         ]
         extra = [((2, 4, H, L), BF16), ((2, 8, L), BF16), ((2, 2, 8, L), I32), ((L, L), BF16)]
         vmem = [pl.BlockSpec(memory_space=pltpu.VMEM)]

time: 47.3 us -> 47 us (level)
  no operation moved by 1% of the time
where the time goes in v5:
time: 47 us; the launch traced here: 46.9 us
  Pallas kernels  46.2 us (98%)
  between operations  0.64 us (1%)
    pallas_call x1, Pallas kernels, local_step(): pl.pallas_call(make_kernel(dp_size), out_shape=[pltpu.VMEM(s, t) for s, t...  42.6 us
    pallas_call x1, Pallas kernels, local_step(): pl.pallas_call(flush_kernel, out_shape=[jax.ShapeDtypeStruct(s, t) for s,...  3.61 us

profile of v5, /device:TPU:0, one launch (start us, length us, event | category | flops | bytes accessed | tf_op | source)
XLA Modules:
  0.0 46.9 jit_solution(346294658500218473)
XLA Ops:
  0.6 42.6 %shard_map.153 = (f32[1,1]{1,0:T(1,128)}, bf16[64,256,128]{2,1,0:T(8,128)(2,1)S(1)}, bf16[4096,256]{1,0:T(8,128)(2,1)S(1)}, f32[64,128]{1,0:T(8,128)S(1)}, f32[1...) custom-call(bf16[64,256,128]{2,1,0:T(8,128)(2,1)} %bitcast.17, ...), custom_call_target="tpu_custom_call" | custom-call | tf_op jit(solution)/shard_map/pallas_call | solution.py:492
  43.2 3.6 %shard_map.154 = (f32[1,1]{1,0:T(1,128)}, bf16[64,256,128]{2,1,0:T(8,128)(2,1)}, bf16[4096,256]{1,0:T(8,128)(2,1)}, f32[64,128]{1,0:T(8,128)}, f32[1,64]{1,0:T(1...) custom-call(f32[1,1]{1,0:T(1,128)} %get-tuple-element.25.loss_i, bf16[64,256,128]{2,1,0:T(8,128)(2,1)S(1)} %get-tuple-element.26.dz_i, ...), custom_call_target="tpu_custom_call" | custom-call | tf_op jit(solution)/shard_map/pallas_call | solution.py:501

commit v6 on v5

--- a/solution.py
+++ b/solution.py
@@ -13,15 +13,17 @@
 MESH = pl.DeviceIdType.MESH
 DSEM = pltpu.SemaphoreType.DMA
 KEEP = True
+CLS = 23
 Q = 32
 EARLY = 4
+SPLIT = (4,)
+SENT, KEPT = True, False
 PEERS = (1, 2, 3)
 FAR = (2, 3)
 BOTH = (0, 1)
 QUARTERS = range(4)
 KIB = 1024
 LAST = 3
-S = 56
 H = 64
 L = 128
 N = 256
@@ -73,8 +75,8 @@
                zv, mv, mask_v, tb_v, mt_v, bm_v, wd_v, bd_v, wm_v, bmb_v,
                wt2, wmt, wmn, bias_c, mbias_c, lab, lts, ltp, ltr, l1n, l2n, t1o, t2o, t1r, t2r, mlab,
                cnt_s, cnt_r, rn, rz, f0, f1, ntn, ntf, vb, vr, db, dbh, dr, dwd_acc, dwm_acc, dbd_acc, dbm_acc, nll_acc,
-               ps, pa, ph, px, pb, pc, pf,
-               lsem, cs, cr, ls, lr, ns, nr, zs, zr, vs, vrs, ds, drs, ars, arr):
+               ps, pa, ph, px, pc, pb, pf, es, ea, eh, ex, ec, eb, ef,
+               lsem, cs, cr, ls, lr, ns, nr, zs, zr, vs, vrs, ds, drs, ars, arr, ready):
         dp = lax.axis_index("dp")
         d = lax.axis_index("dap")
         chip, core = d // 2, d % 2
@@ -98,8 +100,10 @@
         for k in PEERS:
             pl.semaphore_signal(bar, inc=1, device_id=(dp, dap_peer[k]), device_id_type=MESH)
         for k in (1, 2):
-            for there in (d, dap_peer[1]):
-                pl.semaphore_signal(bar, inc=1, device_id=(dp_peer[k], there), device_id_type=MESH)
+            @pl.when(dp_peer[k] > 0)
+            def _():
+                for there in (d, dap_peer[1]):
+                    pl.semaphore_signal(bar, inc=1, device_id=(dp_peer[k], there), device_id_type=MESH)
 
         for n in QUARTERS:
             loc[n].wait()
@@ -107,7 +111,7 @@
         bertf = bm_v[:].astype(F32)
         cd = jnp.sum(jnp.sum(maskf, axis=0, keepdims=KEEP), axis=1, keepdims=KEEP)
         cm = jnp.sum(jnp.sum(bertf, axis=0, keepdims=KEEP), axis=1, keepdims=KEEP)
-        cnt_s[0:8, :] = jnp.broadcast_to(cd, (8, L))
+        cnt_s[:8, :] = jnp.broadcast_to(cd, (8, L))
         cnt_s[8:16, :] = jnp.broadcast_to(cm, (8, L))
         labv = jnp.where(mask_v[:] > 0, tb_v[:], H)
         lab[:] = labv
@@ -117,13 +121,17 @@
         for p in QUARTERS:
             ltp[p] = jnp.where(low, lts[H * p:H * p + Q, :], lts[H * p + Q:H * p + H, :])
 
-        pl.semaphore_wait(bar, 7)
+        pl.semaphore_wait(bar, 3 + 4 * ((dp + 3) // 4))
+        for k in (1, 2):
+            @pl.when(dp_peer[k] == 0)
+            def _():
+                for there in (d, dap_peer[1]):
+                    pl.semaphore_signal(ready, inc=1, device_id=(dp_peer[k], there), device_id_type=MESH)
 
         def rcopy(src, dst, s, r, dpi, dapi):
             return pltpu.make_async_remote_copy(src_ref=src, dst_ref=dst, send_sem=s, recv_sem=r,
                                                 device_id=(dpi, dapi), device_id_type=MESH)
 
-        sends = []
         cc, lc, zc = {}, {}, {}
         for k in (2, 3, 1):
             cc[k] = rcopy(cnt_s, cnt_r.at[k - 1], cs.at[k - 1], cr.at[k - 1], dp, dap_peer[k])
@@ -147,27 +155,27 @@
             loc[n].wait()
         wt = wd_v[:]
         nat = wt.astype(F32).T.astype(BF16)
-        wt2[0:L, :] = nat
+        wt2[:L, :] = nat
         wt2[L:N, :] = nat
-        w2[0:H, :] = wt
+        w2[:H, :] = wt
         w2[H:L, :] = wt
         wmt[:] = jnp.zeros_like(wmt)
-        wmt[0:23, :] = wm_v[:]
+        wmt[:CLS, :] = wm_v[:]
         wmn[:] = wmt[:].astype(F32).T.astype(BF16)
         bias_c[:] = jnp.broadcast_to(row_to_col(bd_v[:], H), (H, L))
-        pad = lax.broadcasted_iota(I32, (32, 1), 0) >= 23
-        mbias_c[:] = jnp.broadcast_to(jnp.where(pad, -1e30, row_to_col(bmb_v[:], 32)), (32, L))
+        pad = lax.broadcasted_iota(I32, (Q, 1), 0) >= CLS
+        mbias_c[:] = jnp.broadcast_to(jnp.where(pad, -1e30, row_to_col(bmb_v[:], Q)), (Q, L))
         l1n[:] = lab[:, pl.ds(near, L)]
         mlv = jnp.where(bm_v[:] > 0, mt_v[:], H)
         bm_v[:] = mlv
-        mlab[:] = jnp.concatenate([bm_v[pl.ds(0, 32, stride=2), :], bm_v[pl.ds(1, 32, stride=2), :]], axis=1)
+        mlab[:] = jnp.concatenate([bm_v[pl.ds(0, Q, stride=2), :], bm_v[pl.ds(1, Q, stride=2), :]], axis=1)
         for a in (dwd_acc, dwm_acc, dbd_acc, dbm_acc, nll_acc):
             a[:] = jnp.zeros_like(a)
 
         for k in PEERS:
             cc[k].wait_recv()
         tot = (cnt_s[:] + cnt_r[0]) + (cnt_r[1] + cnt_r[2])
-        den_d = DIST_EPS + tot[0:1, :]
+        den_d = DIST_EPS + tot[:1, :]
         den_m = MSA_EPS + tot[8:9, :]
         cvd = (LOSS_SCALE * DIST_WEIGHT / batch) / den_d
         cvm = (LOSS_SCALE * MSA_WEIGHT / batch) / den_m
@@ -175,7 +183,7 @@
         cm2 = jnp.concatenate([cvm, cvm], axis=1)
 
         def fold(a):
-            return a[:, 0:L] + a[:, L:N]
+            return a[:, :L] + a[:, L:N]
 
 
         loc[8].wait()
@@ -188,7 +196,7 @@
             mx = jnp.max(l, axis=0, keepdims=KEEP)
             e = jnp.exp(l - mx)
             s = jnp.sum(e, axis=0, keepdims=KEEP)
-            eq = lax.broadcasted_iota(I32, (32, N), 0) == t
+            eq = lax.broadcasted_iota(I32, (Q, N), 0) == t
             mk = (t < H).astype(F32)
             c = cm2 * mk
             h = (e * (c / s) - jnp.where(eq, c, 0.0)).astype(BF16)
@@ -224,20 +232,20 @@
         l1f = lab[:, pl.ds(far, L)].astype(F32)
         for k in FAR:
             a = jnp.where(wide == (dap_peer[k] % 2 == 0), l1f, turn(l1f))
-            t1o[k - 2] = paired(jnp.where(mine_low, a[0:Q, :], a[Q:H, :]))
+            t1o[k - 2] = paired(jnp.where(mine_low, a[:Q, :], a[Q:H, :]))
             got = ltr[k - 1]
             t2o[k - 2] = paired(jnp.where(low == mine_low, got, turn(got)))
             sent = ltp[dap_peer[k]]
             t1r[k - 2] = paired(jnp.where(low == peer_low, sent, turn(sent)))
             u = unpack(got)
             u = jnp.concatenate([u, u], axis=0).T
-            t2r[k - 2] = paired(jnp.where(peer_low, u[0:Q, :], u[Q:H, :]))
+            t2r[k - 2] = paired(jnp.where(peer_low, u[:Q, :], u[Q:H, :]))
             tl_o[0, k - 2] = t1r[k - 2, 8 * LAST:Q, :]
             tl_o[1, k - 2] = t2r[k - 2, 8 * LAST:Q, :]
 
         def swap(src, nt, q, off):
             chunk = src.astype(F32)
-            f0[:] = chunk[:, 0:8, :].reshape(512, L)
+            f0[:] = chunk[:, :8, :].reshape(512, L)
             f1[:] = chunk[:, 8:16, :].reshape(512, L)
             for t in range(8):
                 nt[16 * q + t, pl.ds(off, H), :] = f0[pl.ds(t, H, stride=8), :].astype(BF16)
@@ -266,7 +274,7 @@
             g1 = (e * (c1 / s) - jnp.where(eq1, c1, 0.0)).astype(BF16)
             g2 = (e * (c2 / s) - jnp.where(bins == t2, c2, 0.0)).astype(BF16)
             lt = jnp.sum(jnp.where(eq1, l, 0.0), axis=0, keepdims=KEEP)
-            nll_acc[0:1, :] += fold(m1 * lse - lt)
+            nll_acc[:1, :] += fold(m1 * lse - lt)
             dbd_acc[:] += fold(g1.astype(F32))
             g = jnp.concatenate([g1, g2], axis=0)
             dz_o[pl.ds(2 * i, 2), pl.ds(near, L), :] = dot(g, w2[:], 0, 0).astype(BF16).reshape(2, L, L)
@@ -276,7 +284,7 @@
         def own_tiles(k, q):
             for b in BOTH:
                 zc[k, q, b].wait_recv()
-                f0[0:N, :] = rz[k - 2, q, b].astype(F32).reshape(N, L)
+                f0[:N, :] = rz[k - 2, q, b].astype(F32).reshape(N, L)
                 for t in range(8):
                     r = H * (t // 4) + Q * b
                     ntf[k - 2, 4 * q + t % 4, r:r + Q, :] = f0[pl.ds(t, Q, stride=8), :].astype(BF16)
@@ -300,7 +308,7 @@
                 g1 = (jnp.where(eq1, w, v) * m1).astype(BF16)
                 g2 = (jnp.where(eq2, w, v) * m2).astype(BF16)
                 lt = jnp.sum(jnp.where(eq1, l, 0.0) + jnp.where(eq2, l, 0.0), axis=0, keepdims=KEEP)
-                nll_acc[0:1, :] += fold((m1 + m2) * lse - lt)
+                nll_acc[:1, :] += fold((m1 + m2) * lse - lt)
                 dbd_acc[:] += fold(g1.astype(F32) + g2.astype(F32))
                 vh = v.astype(BF16)
                 for tt in BOTH:
@@ -320,12 +328,21 @@
 
         vc, dc = {}, {}
 
-        def give(k, q):
-            v_to, d_to = (vr.at[k - 2, q], dr.at[k - 2, q]) if q < LAST else (vl_o.at[k - 2], dl_o.at[k - 2])
-            vc[k, q] = rcopy(vb.at[k - 2, q], v_to, vs.at[k - 2, q], vrs.at[k - 2, q], dp, dap_peer[k])
-            dc[k, q] = rcopy(dbh.at[k - 2, q], d_to, ds.at[k - 2, q], drs.at[k - 2, q], dp, dap_peer[k])
-            vc[k, q].start()
-            dc[k, q].start()
+        def give(k, q, when):
+            unit = 2 * q + k - 2
+            if when == SENT:
+                v_to, d_to = (vr.at[k - 2, q], dr.at[k - 2, q]) if q < LAST else (vl_o.at[k - 2], dl_o.at[k - 2])
+                vc[k, q] = rcopy(vb.at[k - 2, q], v_to, vs.at[k - 2, q], vrs.at[k - 2, q], dp, dap_peer[k])
+                dc[k, q] = rcopy(dbh.at[k - 2, q], d_to, ds.at[k - 2, q], drs.at[k - 2, q], dp, dap_peer[k])
+
+            def start():
+                vc[k, q].start()
+                dc[k, q].start()
+
+            if (unit < EARLY) == when and unit not in SPLIT:
+                start()
+            if unit in SPLIT:
+                pl.when((dp == 0) if when == SENT else (dp > 0))(start)
 
         def take(k, q):
             vc[k, q].wait_recv()
@@ -333,7 +350,55 @@
             returned_pairs(vr.at[k - 2, q], dr.at[k - 2, q], t1r.at[k - 2], t2r.at[k - 2], 4 * q, w2, f0, f1)
             for b, f in ((0, f0), (1, f1)):
                 cols = pl.multiple_of(base[k] + Q * phalf[b] + 8 * q, 8)
-                dz_o[Q * b:Q * b + Q, pl.ds(cols, 8), :] = f[0:N, :].reshape(Q, 8, L).astype(BF16)
+                dz_o[Q * b:Q * b + Q, pl.ds(cols, 8), :] = f[:N, :].reshape(Q, 8, L).astype(BF16)
+
+        def reduction(src, ra, rh, rx, rc, rb, full, first):
+            n = rh.shape[0]
+            mine = pl.ds(pl.multiple_of(n * core, 8), n)
+            other = pl.ds(pl.multiple_of(n * (1 - core), 8), n)
+
+            def trio(halves, a, dst, sem, k):
+                there = ((dp, dap_peer[1]), (dp_peer[k], d), (dp_peer[k], dap_peer[1]))
+                group = [rcopy(a.at[rows, :], dst.at[m], ars.at[sem + m], arr.at[sem + m], *to)
+                         for m, (rows, to) in enumerate(zip(halves, there))]
+                for c in group:
+                    c.start()
+                return group
+
+            one = trio((other, mine, other), src, ra, first, 1)
+            yield
+            for c in one:
+                c.wait_recv()
+            rh[:] = (src[mine, :] + ra[0]) + (ra[1] + ra[2])
+            two = rcopy(rh, rx, ars.at[first + 6], arr.at[first + 6], dp, dap_peer[2])
+            two.start()
+            yield
+            two.wait_recv()
+            rc[:] = rh[:] + rx[:]
+            three = trio((pl.ds(0, n),) * 3, rc, rb, first + 3, 2)
+            yield
+            for c in three:
+                c.wait_recv()
+            full[mine, :] = rc[:] + rb[1]
+            full[other, :] = rb[0] + rb[2]
+            for c in (*one, two, *three):
+                c.wait_send()
+            yield
+
+        end = lax.broadcasted_iota(I32, (1, L), 1) == L - 1
+        es[:CLS, :] = dwm_acc[:CLS, :L]
+        es[CLS:2 * CLS, :] = dwm_acc[:CLS, L:N]
+        nm = jnp.sum(nll_acc[1:2, :], axis=1, keepdims=KEEP)
+        part = MSA_WEIGHT * nm / den_m / batch
+        es[2 * CLS:47, :] = col_to_row(jnp.sum(dbm_acc[:], axis=1, keepdims=KEEP), L) + jnp.where(end, part, 0.0)
+        es[47:48, :] = jnp.zeros((1, L), F32)
+
+        @pl.when(dp == 0)
+        def _():
+            pl.semaphore_wait(ready, 4)
+
+        soon = reduction(es, ea, eh, ex, ec, eb, ef, 7)
+        next(soon)
 
         own_off = pl.multiple_of(H * core, H)
         oth_off = pl.multiple_of(H * (1 - core), H)
@@ -343,77 +408,53 @@
         for q in QUARTERS:
             nc[q].wait_recv()
             swap(rn[q], ntn, q, oth_off)
-        lax.fori_loop(0, 32, near_tile, 0, unroll=4)
-
+        lax.fori_loop(0, Q, near_tile, 0, unroll=4)
+
+        next(soon)
         for q in QUARTERS:
             for k in FAR:
                 own_tiles(k, q)
-                if 2 * q + k - 2 < EARLY:
-                    give(k, q)
-
-        ps[0:H, :] = dwd_acc[0:H, :] + dwd_acc[H:L, :]
-        ps[H:87, :] = dwm_acc[0:23, 0:L]
-        ps[87:110, :] = dwm_acc[0:23, L:N]
-        nd = jnp.sum(nll_acc[0:1, :], axis=1, keepdims=KEEP)
-        nm = jnp.sum(nll_acc[1:2, :], axis=1, keepdims=KEEP)
-        part = (DIST_WEIGHT * nd / den_d + MSA_WEIGHT * nm / den_m) / batch
-        dbd = col_to_row(jnp.sum(dbd_acc[:], axis=1, keepdims=KEEP), L)
-        dbm = col_to_row(jnp.sum(dbm_acc[:], axis=1, keepdims=KEEP), L)
-        end = lax.broadcasted_iota(I32, (1, L), 1) == L - 1
-        ps[110:111, :] = dbd + turn(dbm) + jnp.where(end, part, 0.0)
-        ps[111:112, :] = jnp.zeros((1, L), F32)
-
-        mine = pl.ds(pl.multiple_of(S * core, S), S)
-        other = pl.ds(pl.multiple_of(S * (1 - core), S), S)
-        def trio(halves, src, dst, first, k):
-            there = ((dp, dap_peer[1]), (dp_peer[k], d), (dp_peer[k], dap_peer[1]))
-            group = [rcopy(src.at[rows, :], dst.at[n], ars.at[first + n], arr.at[first + n], *to)
-                     for n, (rows, to) in enumerate(zip(halves, there))]
-            for c in group:
-                c.start()
-            return group
-
-        sums = trio((other, mine, other), ps, pa, 0, 1)
-        for c in sums:
-            c.wait_recv()
-        ph[:] = (ps[mine, :] + pa[0]) + (pa[1] + pa[2])
-        cx = rcopy(ph, px, ars.at[6], arr.at[6], dp, dap_peer[2])
-        cx.start()
+                give(k, q, SENT)
+
+        wd = ps.shape[0]
+        ps[:H, :] = dwd_acc[:H, :] + dwd_acc[H:L, :]
+        ps[H:wd, :] = jnp.zeros((wd - H, L), F32)
+        nd = jnp.sum(nll_acc[:1, :], axis=1, keepdims=KEEP)
+        part = DIST_WEIGHT * nd / den_d / batch
+        ps[H:H + 1, :] = col_to_row(jnp.sum(dbd_acc[:], axis=1, keepdims=KEEP), L) + jnp.where(end, part, 0.0)
+        late = reduction(ps, pa, ph, px, pc, pb, pf, 0)
+        next(late)
+        next(soon)
+        next(late)
         for q in QUARTERS:
             for k in FAR:
-                if 2 * q + k - 2 >= EARLY:
-                    give(k, q)
+                give(k, q, KEPT)
         for k in FAR:
             take(k, 0)
-        cx.wait_recv()
-        pc[:] = ph[:] + px[:]
-        everything = pl.ds(0, S)
-        last_sums = trio((everything,) * 3, pc, pb, 3, 2)
+        next(soon)
+        next(late)
         for k in FAR:
             take(k, 1)
-        for c in last_sums:
-            c.wait_recv()
-        pf[mine, :] = pc[:] + pb[1]
-        pf[other, :] = pb[0] + pb[2]
+        next(late)
         for k in FAR:
             take(k, 2)
         for k in FAR:
             vc[k, LAST].wait_recv()
             dc[k, LAST].wait_recv()
-        dwd_o[:] = pf[0:H, :]
-        dwm_o[:, 0:L] = pf[H:87, :]
-        dwm_o[:, L:N] = pf[87:110, :]
-        row = pf[110:111, :]
-        dbd_o[:] = row[:, 0:H]
-        dbm_o[:] = turn(row)[:, 0:23]
-        loss_o[:] = pltpu.roll(row, 1, 1)[:, 0:1]
+        dwd_o[:] = pf[:H, :]
+        dwm_o[:, :L] = ef[:CLS, :]
+        dwm_o[:, L:N] = ef[CLS:2 * CLS, :]
+        row = pf[H:H + 1, :]
+        mrow = ef[2 * CLS:47, :]
+        dbd_o[:] = row[:, :H]
+        dbm_o[:] = mrow[:, :CLS]
+        loss_o[:] = pltpu.roll(row + mrow, 1, 1)[:, :1]
 
         for k in PEERS:
             cc[k].wait_send()
             lc[k].wait_send()
-        for c in (*nc.values(), *zc.values(), *vc.values(), *dc.values(), *sums, *last_sums):
+        for c in (*nc.values(), *zc.values(), *vc.values(), *dc.values()):
             c.wait_send()
-        cx.wait_send()
 
     return kernel
 
@@ -433,6 +474,8 @@
     def put_dz(r, rows, c, cols):
         put(dz_i.at[pl.ds(r, rows), pl.ds(c, cols), :], dz_o.at[pl.ds(r, rows), pl.ds(c, cols), :])
 
+    for n in QUARTERS:
+        put(dm_i.at[pl.ds(KIB * n, KIB), :], dm_o.at[pl.ds(KIB * n, KIB), :])
     for n in QUARTERS:
         put_dz(16 * n, 16, pl.multiple_of(L * chip, L), L)
     spots = {}
@@ -443,8 +486,6 @@
             put_dz(Q * b, Q, mid, 24)
             put_dz(Q * b, Q, pl.multiple_of(start + Q * phalf[1 - b], Q), Q)
             spots[k, b] = pl.multiple_of(mid + 24, 8)
-    for n in QUARTERS:
-        put(dm_i.at[pl.ds(KIB * n, KIB), :], dm_o.at[pl.ds(KIB * n, KIB), :])
     for src, dst in ((loss_i, loss_o), (dwd_i, dwd_o), (dbd_i, dbd_o), (dwm_i, dwm_o), (dbm_i, dbm_o)):
         put(src, dst)
     for k in BOTH:
@@ -466,25 +507,25 @@
 
     def local_step(z, mask, tb, m, mt, bm, wd, bd, wm, bmb):
         args = (z.reshape(H, N, L), mask.reshape(H, N), tb.reshape(H, N), m.reshape(4096, N),
-                mt.reshape(H, H), bm.reshape(H, H), wd.T, bd.reshape(1, H), wm.T, bmb.reshape(1, 23))
+                mt.reshape(H, H), bm.reshape(H, H), wd.T, bd.reshape(1, H), wm.T, bmb.reshape(1, CLS))
         args = tuple(pltpu.with_memory_space_constraint(a, pltpu.HBM) for a in args)
         shapes = [((1, 1), F32), ((H, N, L), BF16), ((4096, N), BF16), ((H, L), F32), ((1, H), F32),
-                  ((23, N), F32), ((1, 23), F32)]
+                  ((CLS, N), F32), ((1, CLS), F32)]
         scratch = [
             V((H, N, L), BF16), V((4096, N), BF16), *[V((H, N), I32)] * 2, V((H, H), I32),
-            V((H, H), I32), V((H, L), BF16), V((1, H), F32), V((23, N), BF16), V((1, 23), F32),
-            V((N, H), BF16), V((32, N), BF16), V((N, 32), BF16), V((H, L), F32), V((32, L), F32),
+            V((H, H), I32), V((H, L), BF16), V((1, H), F32), V((CLS, N), BF16), V((1, CLS), F32),
+            V((N, H), BF16), V((Q, N), BF16), V((N, Q), BF16), V((H, L), F32), V((Q, L), F32),
             V((H, N), I32), V((N, L), F32), V((4, Q, L), F32), V((3, Q, L), F32), V((H, L), I32), V((H, L), I32),
-            *[V((2, Q, L), I32)] * 4, V((32, L), I32),
+            *[V((2, Q, L), I32)] * 4, V((Q, L), I32),
             V((16, L), F32), V((3, 16, L), F32), V((4, H, 16, L), BF16), V((2, 4, 2, Q, 8, L), BF16),
             V((512, L), F32), V((512, L), F32), V((H, L, L), BF16), V((2, 16, L, L), BF16),
             V((2, 4, 4, H, L), BF16), V((2, 3, 4, H, L), BF16), V((2, 4, 8, L), F32), V((2, 4, 8, L), BF16), V((2, 3, 8, L), BF16),
-            V((L, L), F32), V((32, N), F32), V((H, L), F32), V((32, L), F32), V((8, L), F32),
-            V((2 * S, L), F32), V((3, S, L), F32), V((S, L), F32), V((S, L), F32), V((3, S, L), F32), V((S, L), F32),
-            V((2 * S, L), F32),
+            V((L, L), F32), V((Q, N), F32), V((H, L), F32), V((Q, L), F32), V((8, L), F32),
+            *(V((*lead, rows * n, L), F32) for n in (40, 24)
+              for lead, rows in (((), 2), ((3,), 1), ((), 1), ((), 1), ((), 1), ((3,), 1), ((), 2))),
             DSEM((10,)), *[DSEM((3,))] * 4, DSEM((4,)), DSEM((4,)),
             *[DSEM((2, 4, 2))] * 2, *[DSEM((2, 4))] * 4,
-            DSEM((7,)), DSEM((7,)),
+            *[DSEM((14,))] * 2, pltpu.SemaphoreType.REGULAR,
         ]
         extra = [((2, 4, H, L), BF16), ((2, 8, L), BF16), ((2, 2, 8, L), I32), ((L, L), BF16)]
         vmem = [pl.BlockSpec(memory_space=pltpu.VMEM)]
@@ -508,7 +549,7 @@
         )(*outs)
         loss, dz, dm, dwd, dbd, dwm, dbm = outs
         return (loss.reshape(()), dz.reshape(1, H, N, L), dm.reshape(1, H, H, N), dwd.T, dbd.reshape(H),
-                dwm.T, dbm.reshape(23))
+                dwm.T, dbm.reshape(CLS))
 
     return jax.shard_map(local_step, mesh=mesh,
                          in_specs=(pair_spec, pair_int_spec, pair_int_spec, msa_spec, msa_int_spec, msa_int_spec,

time: 47 us -> 46.2 us (0.983)
  Pallas kernels: 46.2 us -> 45.5 us
    pallas_call x1, Pallas kernels: 42.6 us -> 42 us  [local_step(): pl.pallas_call(make_kernel(dp_size), out_shape=[pltpu.VMEM(s, t) for s, t...]
where the time goes in v6:
time: 46.2 us; the launch traced here: 46.1 us
  Pallas kernels  45.5 us (98%)
  between operations  0.64 us (1%)
    pallas_call x1, Pallas kernels, local_step(): pl.pallas_call(make_kernel(dp_size), out_shape=[pltpu.VMEM(s, t) for s, t...  42 us
    pallas_call x1, Pallas kernels, local_step(): pl.pallas_call(flush_kernel, out_shape=[jax.ShapeDtypeStruct(s, t) for s,...  3.5 us

profile of v6, /device:TPU:0, one launch (start us, length us, event | category | flops | bytes accessed | tf_op | source)
XLA Modules:
  0.0 46.1 jit_solution(16326504417163619642)
XLA Ops:
  0.6 42.0 %shard_map.153 = (f32[1,1]{1,0:T(1,128)}, bf16[64,256,128]{2,1,0:T(8,128)(2,1)S(1)}, bf16[4096,256]{1,0:T(8,128)(2,1)S(1)}, f32[64,128]{1,0:T(8,128)S(1)}, f32[1...) custom-call(bf16[64,256,128]{2,1,0:T(8,128)(2,1)} %bitcast.17, ...), custom_call_target="tpu_custom_call" | custom-call | tf_op jit(solution)/shard_map/pallas_call | solution.py:533
  42.6 3.5 %shard_map.154 = (f32[1,1]{1,0:T(1,128)}, bf16[64,256,128]{2,1,0:T(8,128)(2,1)}, bf16[4096,256]{1,0:T(8,128)(2,1)}, f32[64,128]{1,0:T(8,128)}, f32[1,64]{1,0:T(1...) custom-call(f32[1,1]{1,0:T(1,128)} %get-tuple-element.25.loss_i, bf16[64,256,128]{2,1,0:T(8,128)(2,1)S(1)} %get-tuple-element.26.dz_i, ...), custom_call_target="tpu_custom_call" | custom-call | tf_op jit(solution)/shard_map/pallas_call | solution.py:542

commit v7 on v6

--- a/solution.py
+++ b/solution.py
@@ -435,9 +435,9 @@
         next(late)
         for k in FAR:
             take(k, 1)
-        next(late)
         for k in FAR:
             take(k, 2)
+        next(late)
         for k in FAR:
             vc[k, LAST].wait_recv()
             dc[k, LAST].wait_recv()

time: 46.2 us -> 46.1 us (level)
  no operation moved by 1% of the time
where the time goes in v7:
time: 46.1 us; the launch traced here: 46 us
  Pallas kernels  45.3 us (98%)
  between operations  0.64 us (1%)
    pallas_call x1, Pallas kernels, local_step(): pl.pallas_call(make_kernel(dp_size), out_shape=[pltpu.VMEM(s, t) for s, t...  41.8 us
    pallas_call x1, Pallas kernels, local_step(): pl.pallas_call(flush_kernel, out_shape=[jax.ShapeDtypeStruct(s, t) for s,...  3.5 us

profile of v7, /device:TPU:0, one launch (start us, length us, event | category | flops | bytes accessed | tf_op | source)
XLA Modules:
  0.0 46.0 jit_solution(10782281388937100797)
XLA Ops:
  0.6 41.8 %shard_map.153 = (f32[1,1]{1,0:T(1,128)}, bf16[64,256,128]{2,1,0:T(8,128)(2,1)S(1)}, bf16[4096,256]{1,0:T(8,128)(2,1)S(1)}, f32[64,128]{1,0:T(8,128)S(1)}, f32[1...) custom-call(bf16[64,256,128]{2,1,0:T(8,128)(2,1)} %bitcast.17, ...), custom_call_target="tpu_custom_call" | custom-call | tf_op jit(solution)/shard_map/pallas_call | solution.py:533
  42.5 3.5 %shard_map.154 = (f32[1,1]{1,0:T(1,128)}, bf16[64,256,128]{2,1,0:T(8,128)(2,1)}, bf16[4096,256]{1,0:T(8,128)(2,1)}, f32[64,128]{1,0:T(8,128)}, f32[1,64]{1,0:T(1...) custom-call(f32[1,1]{1,0:T(1,128)} %get-tuple-element.25.loss_i, bf16[64,256,128]{2,1,0:T(8,128)(2,1)S(1)} %get-tuple-element.26.dz_i, ...), custom_call_target="tpu_custom_call" | custom-call | tf_op jit(solution)/shard_map/pallas_call | solution.py:542

commit v8 on v7

--- a/solution.py
+++ b/solution.py
@@ -52,11 +52,11 @@
     return jnp.concatenate([ref[pl.ds(2 * i, 1), :], ref[pl.ds(2 * i + 1, 1), :]], axis=1)
 
 
-def returned_pairs(v_ref, d_ref, mine, peers, first, w2, f0, f1):
+def returned_pairs(v_ref, mine, peers, first, w2, f0, f1):
     bins = lax.broadcasted_iota(I32, (H, N), 0)
-    dv = d_ref[:].astype(F32)
+    dv = v_ref[N:, :].astype(F32)
     for j in BOTH:
-        v = jnp.concatenate([v_ref[2 * j], v_ref[2 * j + 1]], axis=1).astype(F32)
+        v = jnp.concatenate([v_ref[L * j:L * j + H, :], v_ref[L * j + H:L * j + L, :]], axis=1).astype(F32)
         gs = []
         for table, row in ((mine, 4 + 2 * j), (peers, 2 * j)):
             t = lanes2(table, first + j)
@@ -71,12 +71,12 @@
 
 def make_kernel(batch):
     def kernel(z_h, mask_h, tb_h, m_h, mt_h, bm_h, wd_h, bd_h, wm_h, bmb_h,
-               loss_o, dz_o, dm_o, dwd_o, dbd_o, dwm_o, dbm_o, vl_o, dl_o, tl_o, w2,
+               loss_o, dz_o, dm_o, dwd_o, dbd_o, dwm_o, dbm_o, vl_o, tl_o, w2,
                zv, mv, mask_v, tb_v, mt_v, bm_v, wd_v, bd_v, wm_v, bmb_v,
                wt2, wmt, wmn, bias_c, mbias_c, lab, lts, ltp, ltr, l1n, l2n, t1o, t2o, t1r, t2r, mlab,
-               cnt_s, cnt_r, rn, rz, f0, f1, ntn, ntf, vb, vr, db, dbh, dr, dwd_acc, dwm_acc, dbd_acc, dbm_acc, nll_acc,
+               cnt_s, cnt_r, rn, rz, f0, f1, ntn, ntf, vb, vr, db, dwd_acc, dwm_acc, dbd_acc, dbm_acc, nll_acc,
                ps, pa, ph, px, pc, pb, pf, es, ea, eh, ex, ec, eb, ef,
-               lsem, cs, cr, ls, lr, ns, nr, zs, zr, vs, vrs, ds, drs, ars, arr, ready):
+               lsem, cs, cr, ls, lr, ns, nr, zs, zr, vs, vrs, ars, arr, ready):
         dp = lax.axis_index("dp")
         d = lax.axis_index("dap")
         chip, core = d // 2, d % 2
@@ -313,7 +313,7 @@
                 vh = v.astype(BF16)
                 for tt in BOTH:
                     cut = slice(L * tt, L * tt + L)
-                    vb[k - 2, q, 2 * j + tt] = vh[:, cut]
+                    vb[k - 2, q, pl.ds(pl.multiple_of(L * j + H * tt, H), H), :] = vh[:, cut]
                     db[k - 2, q, pl.ds(2 * j + tt, 1), :] = d1[:, cut]
                     db[k - 2, q, pl.ds(4 + 2 * j + tt, 1), :] = d2[:, cut]
                 g = jnp.concatenate([g1, g2], axis=0)
@@ -324,20 +324,18 @@
                 return carry
 
             lax.fori_loop(0, 2, body, 0, unroll=2)
-            dbh[k - 2, q] = db[k - 2, q].astype(BF16)
-
-        vc, dc = {}, {}
+            vb[k - 2, q, N:, :] = db[k - 2, q].astype(BF16)
+
+        vc = {}
 
         def give(k, q, when):
             unit = 2 * q + k - 2
             if when == SENT:
-                v_to, d_to = (vr.at[k - 2, q], dr.at[k - 2, q]) if q < LAST else (vl_o.at[k - 2], dl_o.at[k - 2])
+                v_to = vr.at[k - 2, q] if q < LAST else vl_o.at[k - 2]
                 vc[k, q] = rcopy(vb.at[k - 2, q], v_to, vs.at[k - 2, q], vrs.at[k - 2, q], dp, dap_peer[k])
-                dc[k, q] = rcopy(dbh.at[k - 2, q], d_to, ds.at[k - 2, q], drs.at[k - 2, q], dp, dap_peer[k])
 
             def start():
                 vc[k, q].start()
-                dc[k, q].start()
 
             if (unit < EARLY) == when and unit not in SPLIT:
                 start()
@@ -346,8 +344,7 @@
 
         def take(k, q):
             vc[k, q].wait_recv()
-            dc[k, q].wait_recv()
-            returned_pairs(vr.at[k - 2, q], dr.at[k - 2, q], t1r.at[k - 2], t2r.at[k - 2], 4 * q, w2, f0, f1)
+            returned_pairs(vr.at[k - 2, q], t1r.at[k - 2], t2r.at[k - 2], 4 * q, w2, f0, f1)
             for b, f in ((0, f0), (1, f1)):
                 cols = pl.multiple_of(base[k] + Q * phalf[b] + 8 * q, 8)
                 dz_o[Q * b:Q * b + Q, pl.ds(cols, 8), :] = f[:N, :].reshape(Q, 8, L).astype(BF16)
@@ -440,7 +437,6 @@
         next(late)
         for k in FAR:
             vc[k, LAST].wait_recv()
-            dc[k, LAST].wait_recv()
         dwd_o[:] = pf[:H, :]
         dwm_o[:, :L] = ef[:CLS, :]
         dwm_o[:, L:N] = ef[CLS:2 * CLS, :]
@@ -453,13 +449,13 @@
         for k in PEERS:
             cc[k].wait_send()
             lc[k].wait_send()
-        for c in (*nc.values(), *zc.values(), *vc.values(), *dc.values()):
+        for c in (*nc.values(), *zc.values(), *vc.values()):
             c.wait_send()
 
     return kernel
 
 
-def flush_kernel(loss_i, dz_i, dm_i, dwd_i, dbd_i, dwm_i, dbm_i, vl, dl, tl, w2,
+def flush_kernel(loss_i, dz_i, dm_i, dwd_i, dbd_i, dwm_i, dbm_i, vl, tl, w2,
                  loss_o, dz_o, dm_o, dwd_o, dbd_o, dwm_o, dbm_o, f0, f1, late, sem):
     d = lax.axis_index("dap")
     chip, core = d // 2, d % 2
@@ -489,7 +485,7 @@
     for src, dst in ((loss_i, loss_o), (dwd_i, dwd_o), (dbd_i, dbd_o), (dwm_i, dwm_o), (dbm_i, dbm_o)):
         put(src, dst)
     for k in BOTH:
-        returned_pairs(vl.at[k], dl.at[k], tl.at[0, k], tl.at[1, k], 0, w2, f0, f1)
+        returned_pairs(vl.at[k], tl.at[0, k], tl.at[1, k], 0, w2, f0, f1)
         for b, f in ((0, f0), (1, f1)):
             late[k, b] = f[:].reshape(Q, 8, L).astype(BF16)
             put(late.at[k, b], dz_o.at[pl.ds(Q * b, Q), pl.ds(spots[k, b], 8), :])
@@ -519,22 +515,22 @@
             *[V((2, Q, L), I32)] * 4, V((Q, L), I32),
             V((16, L), F32), V((3, 16, L), F32), V((4, H, 16, L), BF16), V((2, 4, 2, Q, 8, L), BF16),
             V((512, L), F32), V((512, L), F32), V((H, L, L), BF16), V((2, 16, L, L), BF16),
-            V((2, 4, 4, H, L), BF16), V((2, 3, 4, H, L), BF16), V((2, 4, 8, L), F32), V((2, 4, 8, L), BF16), V((2, 3, 8, L), BF16),
+            V((2, 4, N + 8, L), BF16), V((2, 3, N + 8, L), BF16), V((2, 4, 8, L), F32),
             V((L, L), F32), V((Q, N), F32), V((H, L), F32), V((Q, L), F32), V((8, L), F32),
             *(V((*lead, rows * n, L), F32) for n in (40, 24)
               for lead, rows in (((), 2), ((3,), 1), ((), 1), ((), 1), ((), 1), ((3,), 1), ((), 2))),
             DSEM((10,)), *[DSEM((3,))] * 4, DSEM((4,)), DSEM((4,)),
-            *[DSEM((2, 4, 2))] * 2, *[DSEM((2, 4))] * 4,
+            *[DSEM((2, 4, 2))] * 2, *[DSEM((2, 4))] * 2,
             *[DSEM((14,))] * 2, pltpu.SemaphoreType.REGULAR,
         ]
-        extra = [((2, 4, H, L), BF16), ((2, 8, L), BF16), ((2, 2, 8, L), I32), ((L, L), BF16)]
+        extra = [((2, N + 8, L), BF16), ((2, 2, 8, L), I32), ((L, L), BF16)]
         vmem = [pl.BlockSpec(memory_space=pltpu.VMEM)]
         hbm = [pl.BlockSpec(memory_space=pltpu.HBM)]
         outs = pl.pallas_call(
             make_kernel(dp_size),
             out_shape=[pltpu.VMEM(s, t) for s, t in shapes + extra],
             in_specs=hbm * 10,
-            out_specs=vmem * 11,
+            out_specs=vmem * 10,
             scratch_shapes=scratch,
             compiler_params=pltpu.CompilerParams(collective_id=0, has_side_effects=True,
                                                  vmem_limit_bytes=44 * KIB * KIB),
@@ -542,7 +538,7 @@
         outs = pl.pallas_call(
             flush_kernel,
             out_shape=[jax.ShapeDtypeStruct(s, t) for s, t in shapes],
-            in_specs=vmem * 11,
+            in_specs=vmem * 10,
             out_specs=hbm * 7,
             scratch_shapes=[V((N, L), F32), V((N, L), F32), V((2, 2, Q, 8, L), BF16), DSEM((25,))],
             compiler_params=pltpu.CompilerParams(vmem_limit_bytes=8 * KIB * KIB),

time: 46.1 us -> 45.9 us (level)
  no operation moved by 1% of the time
where the time goes in v8:
time: 45.9 us; the launch traced here: 45.8 us
  Pallas kernels  45.2 us (98%)
  between operations  0.64 us (1%)
    pallas_call x1, Pallas kernels, local_step(): pl.pallas_call(make_kernel(dp_size), out_shape=[pltpu.VMEM(s, t) for s, t...  41.7 us
    pallas_call x1, Pallas kernels, local_step(): pl.pallas_call(flush_kernel, out_shape=[jax.ShapeDtypeStruct(s, t) for s,...  3.5 us

profile of v8, /device:TPU:0, one launch (start us, length us, event | category | flops | bytes accessed | tf_op | source)
XLA Modules:
  0.0 45.8 jit_solution(10506209570462992005)
XLA Ops:
  0.6 41.7 %shard_map.153 = (f32[1,1]{1,0:T(1,128)}, bf16[64,256,128]{2,1,0:T(8,128)(2,1)S(1)}, bf16[4096,256]{1,0:T(8,128)(2,1)S(1)}, f32[64,128]{1,0:T(8,128)S(1)}, f32[1...) custom-call(bf16[64,256,128]{2,1,0:T(8,128)(2,1)} %bitcast.17, ...), custom_call_target="tpu_custom_call" | custom-call | tf_op jit(solution)/shard_map/pallas_call | solution.py:529
  42.3 3.5 %shard_map.154 = (f32[1,1]{1,0:T(1,128)}, bf16[64,256,128]{2,1,0:T(8,128)(2,1)}, bf16[4096,256]{1,0:T(8,128)(2,1)}, f32[64,128]{1,0:T(8,128)}, f32[1,64]{1,0:T(1...) custom-call(f32[1,1]{1,0:T(1,128)} %get-tuple-element.24.loss_i, bf16[64,256,128]{2,1,0:T(8,128)(2,1)S(1)} %get-tuple-element.25.dz_i, ...), custom_call_target="tpu_custom_call" | custom-call | tf_op jit(solution)/shard_map/pallas_call | solution.py:538

commit v9 on v8

--- a/solution.py
+++ b/solution.py
@@ -111,8 +111,8 @@
         bertf = bm_v[:].astype(F32)
         cd = jnp.sum(jnp.sum(maskf, axis=0, keepdims=KEEP), axis=1, keepdims=KEEP)
         cm = jnp.sum(jnp.sum(bertf, axis=0, keepdims=KEEP), axis=1, keepdims=KEEP)
-        cnt_s[:8, :] = jnp.broadcast_to(cd, (8, L))
-        cnt_s[8:16, :] = jnp.broadcast_to(cm, (8, L))
+        cnt_s[:1, :] = jnp.broadcast_to(cd, (1, L))
+        cnt_s[1:2, :] = jnp.broadcast_to(cm, (1, L))
         labv = jnp.where(mask_v[:] > 0, tb_v[:], H)
         lab[:] = labv
         labf = labv.astype(F32)
@@ -176,7 +176,7 @@
             cc[k].wait_recv()
         tot = (cnt_s[:] + cnt_r[0]) + (cnt_r[1] + cnt_r[2])
         den_d = DIST_EPS + tot[:1, :]
-        den_m = MSA_EPS + tot[8:9, :]
+        den_m = MSA_EPS + tot[1:2, :]
         cvd = (LOSS_SCALE * DIST_WEIGHT / batch) / den_d
         cvm = (LOSS_SCALE * MSA_WEIGHT / batch) / den_m
         cd2 = jnp.concatenate([cvd, cvd], axis=1)
@@ -513,7 +513,7 @@
             V((N, H), BF16), V((Q, N), BF16), V((N, Q), BF16), V((H, L), F32), V((Q, L), F32),
             V((H, N), I32), V((N, L), F32), V((4, Q, L), F32), V((3, Q, L), F32), V((H, L), I32), V((H, L), I32),
             *[V((2, Q, L), I32)] * 4, V((Q, L), I32),
-            V((16, L), F32), V((3, 16, L), F32), V((4, H, 16, L), BF16), V((2, 4, 2, Q, 8, L), BF16),
+            V((2, L), F32), V((3, 2, L), F32), V((4, H, 16, L), BF16), V((2, 4, 2, Q, 8, L), BF16),
             V((512, L), F32), V((512, L), F32), V((H, L, L), BF16), V((2, 16, L, L), BF16),
             V((2, 4, N + 8, L), BF16), V((2, 3, N + 8, L), BF16), V((2, 4, 8, L), F32),
             V((L, L), F32), V((Q, N), F32), V((H, L), F32), V((Q, L), F32), V((8, L), F32),

time: 45.9 us -> 45.6 us (level)
  no operation moved by 1% of the time
where the time goes in v9:
time: 45.6 us; the launch traced here: 45.5 us
  Pallas kernels  44.9 us (98%)
  between operations  0.64 us (1%)
    pallas_call x1, Pallas kernels, local_step(): pl.pallas_call(make_kernel(dp_size), out_shape=[pltpu.VMEM(s, t) for s, t...  41.4 us
    pallas_call x1, Pallas kernels, local_step(): pl.pallas_call(flush_kernel, out_shape=[jax.ShapeDtypeStruct(s, t) for s,...  3.5 us

profile of v9, /device:TPU:0, one launch (start us, length us, event | category | flops | bytes accessed | tf_op | source)
XLA Modules:
  0.0 45.5 jit_solution(8179277849290954933)
XLA Ops:
  0.6 41.4 %shard_map.153 = (f32[1,1]{1,0:T(1,128)}, bf16[64,256,128]{2,1,0:T(8,128)(2,1)S(1)}, bf16[4096,256]{1,0:T(8,128)(2,1)S(1)}, f32[64,128]{1,0:T(8,128)S(1)}, f32[1...) custom-call(bf16[64,256,128]{2,1,0:T(8,128)(2,1)} %bitcast.17, ...), custom_call_target="tpu_custom_call" | custom-call | tf_op jit(solution)/shard_map/pallas_call | solution.py:529
  42.0 3.5 %shard_map.154 = (f32[1,1]{1,0:T(1,128)}, bf16[64,256,128]{2,1,0:T(8,128)(2,1)}, bf16[4096,256]{1,0:T(8,128)(2,1)}, f32[64,128]{1,0:T(8,128)}, f32[1,64]{1,0:T(1...) custom-call(f32[1,1]{1,0:T(1,128)} %get-tuple-element.24.loss_i, bf16[64,256,128]{2,1,0:T(8,128)(2,1)S(1)} %get-tuple-element.25.dz_i, ...), custom_call_target="tpu_custom_call" | custom-call | tf_op jit(solution)/shard_map/pallas_call | solution.py:538
